TPU v7x, 32 devices: a whole 2x2x4 slice. The times are simulated.
32 devices in a mesh: groups: 2 (over x), sp: 8 (over z, y), fsdp: 2 (over core).
Axes of the slice: x: 2, y: 2, z: 4, core: 2. Of those that a mesh axis runs over, the one named last changes fastest.
Arguments:
- policy_hidden: bfloat16 [4, 256, 4096], P(('groups', 'fsdp'), 'sp'), parts along dimension 0, may hold values from -6 to 6
- policy_queries: bfloat16 [4, 256, 1024], P(('groups', 'fsdp'), 'sp'), parts along dimension 0, may hold values from -512 to 512
- policy_documents: int32 [4, 256], P(('groups', 'fsdp'), 'sp'), parts along dimension 0, may hold values from 0 to 31, never falling along the last dimension, each value on 1 to 128 neighbouring positions
- policy_gain: bfloat16 [4096], P(('sp', 'fsdp')), may hold values from 0.099609375 to 1.8984375
- policy_key_weight: bfloat16 [4096, 512], P(('sp', 'fsdp')), may hold values from -0.09375 to 0.09375
- policy_value_weight: bfloat16 [4096, 512], P(('sp', 'fsdp')), may hold values from -0.09375 to 0.09375
- frozen_hidden: bfloat16 [4, 256, 4096], P(('groups', 'fsdp'), 'sp'), parts along dimension 0, may hold values from -6 to 6
- frozen_queries: bfloat16 [4, 256, 1024], P(('groups', 'fsdp'), 'sp'), parts along dimension 0, may hold values from -512 to 512
- frozen_documents: int32 [4, 256], P(('groups', 'fsdp'), 'sp'), parts along dimension 0, may hold values from 0 to 31, never falling along the last dimension, each value on 1 to 128 neighbouring positions
- frozen_gain: bfloat16 [4096], P(('sp', 'fsdp')), may hold values from 0.099609375 to 1.8984375
- frozen_key_weight: bfloat16 [4096, 512], P(('sp', 'fsdp')), may hold values from -0.09375 to 0.09375
- frozen_value_weight: bfloat16 [4096, 512], P(('sp', 'fsdp')), may hold values from -0.09375 to 0.09375
Outputs:
- policy_mixed: bfloat16 [4, 256, 1024], P(('groups', 'fsdp'), 'sp'), parts along dimension 0
- frozen_mixed: bfloat16 [4, 256, 1024], P(('groups', 'fsdp'), 'sp'), parts along dimension 0
There are 2 independent parts, one for each index of `groups`. A program takes and returns all parts, laid end to end along the dimension named above; an argument that names none is the same for every part. Nothing has to cross between parts.
Inputs may be any that keep to these rules, and one draw needn't show every extreme that they name: `policy_documents`: along each sequence the ids never fall, and each document holds 1 to 128 positions. `frozen_documents`: along each sequence the ids never fall, and each document holds 1 to 128 positions.
All inputs are finite; a program needn't handle non-finite values.
Results may differ from a plain program's by a relative error of at most 0.007.
The roundings to bfloat16 on the way count: a program that leaves them out, or rounds other values in their place, can miss the bound.
Values may be sent and summed in bfloat16 or wider, within the bound.
No kernel may reach another device: no remote copies, remote signals or barrier semaphores. Data moves between devices by JAX's collectives and lax.ppermute only.
A program may use at most 128 MiB of HBM per device.

v0:
```python
import jax
import jax.numpy as jnp
from jax import lax
from jax.sharding import PartitionSpec as P

HEAD_DIM = 128


EPS = 1e-05
ROPE_BASE = 500000.0
MASKED = -1e30


def rotate(raw_keys, positions):
    half_dim = HEAD_DIM // 2
    frequency = jnp.exp(
        -jnp.log(ROPE_BASE) * jnp.arange(half_dim, dtype=jnp.float32) * 2.0 / HEAD_DIM
    )
    angles = positions.astype(jnp.float32)[:, None] * frequency[None, :]
    cosines = jnp.cos(angles)[:, None, :]
    sines = jnp.sin(angles)[:, None, :]
    front_half = raw_keys[..., :half_dim]
    back_half = raw_keys[..., half_dim:]
    return jnp.concatenate(
        [front_half * cosines - back_half * sines, back_half * cosines + front_half * sines],
        axis=-1,
    )


def project(hidden, gain, key_weight, value_weight):
    tokens = hidden.shape[1]
    widened = hidden[0].astype(jnp.float32)
    inverse = lax.rsqrt(jnp.mean(widened * widened, axis=-1, keepdims=True) + EPS)
    scaled = widened * inverse
    gain_rows = lax.all_gather(gain, ("sp", "fsdp"), axis=0, tiled=True)
    key_rows = lax.all_gather(key_weight, ("sp", "fsdp"), axis=0, tiled=True)
    value_rows = lax.all_gather(value_weight, ("sp", "fsdp"), axis=0, tiled=True)
    normed = (scaled * gain_rows.astype(jnp.float32)[None, :]).astype(jnp.bfloat16)
    raw_keys = jnp.dot(normed, key_rows, preferred_element_type=jnp.float32)
    raw_values = jnp.dot(normed, value_rows, preferred_element_type=jnp.float32)
    positions = lax.axis_index("sp") * tokens + jnp.arange(tokens, dtype=jnp.int32)
    key_heads = rotate(raw_keys.reshape(tokens, -1, HEAD_DIM), positions).astype(jnp.bfloat16)
    value_heads = raw_values.astype(jnp.bfloat16).reshape(tokens, -1, HEAD_DIM)
    return (key_heads, value_heads)


def attend(queries, key_heads, value_heads, documents):
    length = queries.shape[0]
    head_count = queries.shape[1]
    block_rows = min(512, length)
    margin = min(512, length // 2)
    window = block_rows + margin
    factor = HEAD_DIM ** (-0.5)
    offsets = jnp.arange(block_rows, dtype=jnp.int32)
    window_offsets = jnp.arange(window, dtype=jnp.int32)
    padding = jnp.zeros((margin, head_count, HEAD_DIM), jnp.bfloat16)
    padded_keys = jnp.concatenate([padding, key_heads], axis=0)
    padded_values = jnp.concatenate([padding, value_heads], axis=0)
    padded_docs = jnp.concatenate([jnp.full((margin,), -1, jnp.int32), documents], axis=0)

    def one_block(block_index):
        first = block_index * block_rows
        query_block = lax.dynamic_slice_in_dim(queries, first, block_rows, 0)
        query_docs = lax.dynamic_slice_in_dim(documents, first, block_rows, 0)
        query_positions = first + offsets
        key_block = lax.dynamic_slice_in_dim(padded_keys, first, window, 0)
        value_block = lax.dynamic_slice_in_dim(padded_values, first, window, 0)
        key_docs = lax.dynamic_slice_in_dim(padded_docs, first, window, 0)
        key_positions = first - margin + window_offsets
        allowed = (key_positions[None, :] <= query_positions[:, None]) & (
            key_docs[None, :] == query_docs[:, None]
        )
        scores = (
            jnp.einsum("qnd,knd->nqk", query_block, key_block, preferred_element_type=jnp.float32)
            * factor
        )
        scores = jnp.where(allowed[None], scores, MASKED)
        highest = jnp.max(scores, axis=-1, keepdims=True)
        exponent = jnp.where(allowed[None], jnp.exp(scores - highest), 0.0)
        weights = (exponent / jnp.sum(exponent, axis=-1, keepdims=True)).astype(jnp.bfloat16)
        blended = jnp.einsum(
            "nqk,knd->qnd", weights, value_block, preferred_element_type=jnp.float32
        )
        return blended.astype(jnp.bfloat16)

    blocks = lax.map(one_block, jnp.arange(length // block_rows, dtype=jnp.int32))
    return blocks.reshape(length, head_count, HEAD_DIM)


def run_model(hidden, queries, documents, gain, key_weight, value_weight):
    tokens = hidden.shape[1]
    head_count = queries.shape[2] // HEAD_DIM
    query_local = queries[0].reshape(tokens, head_count, HEAD_DIM)
    every_doc = lax.all_gather(documents[0], "sp", axis=0, tiled=True)
    key_heads, value_heads = project(hidden, gain, key_weight, value_weight)
    group_size = head_count // key_heads.shape[1]
    wide_keys = jnp.repeat(key_heads, group_size, axis=1)
    wide_values = jnp.repeat(value_heads, group_size, axis=1)
    query_spread, key_spread, value_spread = (
        lax.all_to_all(query_local, "sp", split_axis=1, concat_axis=0, tiled=True),
        lax.all_to_all(wide_keys, "sp", split_axis=1, concat_axis=0, tiled=True),
        lax.all_to_all(wide_values, "sp", split_axis=1, concat_axis=0, tiled=True),
    )
    mixed = attend(query_spread, key_spread, value_spread, every_doc)
    returned = lax.all_to_all(mixed, "sp", split_axis=0, concat_axis=1, tiled=True)
    return returned.reshape(1, tokens, head_count * HEAD_DIM)


def per_device(
    policy_hidden,
    policy_queries,
    policy_documents,
    policy_gain,
    policy_key_weight,
    policy_value_weight,
    frozen_hidden,
    frozen_queries,
    frozen_documents,
    frozen_gain,
    frozen_key_weight,
    frozen_value_weight,
):
    policy_mixed = run_model(
        policy_hidden,
        policy_queries,
        policy_documents,
        policy_gain,
        policy_key_weight,
        policy_value_weight,
    )
    frozen_mixed = run_model(
        frozen_hidden,
        frozen_queries,
        frozen_documents,
        frozen_gain,
        frozen_key_weight,
        frozen_value_weight,
    )
    return (policy_mixed, frozen_mixed)


def solution(mesh):
    return jax.shard_map(
        per_device,
        mesh=mesh,
        in_specs=(
            P(("groups", "fsdp"), "sp", None),
            P(("groups", "fsdp"), "sp", None),
            P(("groups", "fsdp"), "sp"),
            P(("sp", "fsdp")),
            P(("sp", "fsdp"), None),
            P(("sp", "fsdp"), None),
            P(("groups", "fsdp"), "sp", None),
            P(("groups", "fsdp"), "sp", None),
            P(("groups", "fsdp"), "sp"),
            P(("sp", "fsdp")),
            P(("sp", "fsdp"), None),
            P(("sp", "fsdp"), None),
        ),
        out_specs=(P(("groups", "fsdp"), "sp", None), P(("groups", "fsdp"), "sp", None)),
        check_vma=False,
    )
```

profile of v0, /device:TPU:0, one launch (start us, length us, event | category | flops | bytes accessed | tf_op | source)
XLA Modules:
  0.0 280.7 jit_solution(6077862936525834880)
XLA Ops:
  11.5 7.3 %all-to-all-start.6 = ((bf16[32,8,128]{2,0,1:T(8,128)(2,1)}), bf16[32,8,128]{2,0,1:T(8,128)(2,1)S(1)}, u32[]{:S(2)}, u32[]{:S(2)}) async-start(bf16[32,8,128]{2,0,1:T(8,128)(2,1)} %copy.43), calls=%async_computation.6 | async-start | bytes 131072 | tf_op jit(solution)/shard_map/all_to_all | solution.py:100
  19.4 21.8 %all-gather.3 = bf16[16,1,256]{2,1,0:T(2,128)(2,1)S(1)} all-gather(bf16[1,1,256]{2,1,0:T(2,128)(2,1)S(1)} %reshape.242), channel_id=1, replica_groups=mesh['groups'=2,'sp'=8,'fsdp'=2] {'sp','fsdp'}, dimensions={0}, use_global_device_ids=true | all-gather | bytes 8704 | tf_op jit(solution)/shard_map/all_gather | solution.py:35
  41.9 17.8 %all-gather.2 = bf16[16,1,256]{2,1,0:T(2,128)(2,1)S(1)} all-gather(bf16[1,1,256]{2,1,0:T(2,128)(2,1)S(1)} %reshape.240), channel_id=1, replica_groups=mesh['groups'=2,'sp'=8,'fsdp'=2] {'sp','fsdp'}, dimensions={0}, use_global_device_ids=true | all-gather | bytes 8704 | tf_op jit(solution)/shard_map/all_gather | solution.py:35
  63.1 8.1 %all-reduce.8 = (s32[256]{0:T(256)S(1)}, s32[256]{0:T(256)S(1)}) all-reduce(s32[256]{0:T(256)S(1)} %bitcast_dynamic-update-slice_fusion.1, s32[256]{0:T(256)S(1)} %bitcast_dynamic-update-slice_fusion), channel_id=2, replica_groups=mesh['groups'=2,'sp'=8,'fsdp'=2] {'sp'}, use_global_device_ids=true, to_apply=%add.6 | all-reduce | flops 512 | bytes 4096 | tf_op jit(solution)/shard_map/all_gather | solution.py:94
  75.2 6.4 %copy.42 = bf16[512,4096]{1,0:T(8,128)(2,1)} copy(bf16[512,4096]{0,1:T(8,128)(2,1)} %bitcast.149) | data formatting | bytes 8388608 | tf_op jit(solution)/shard_map/dot_general | solution.py:39
  81.6 33.1 %all-gather.11.cloned.1.call-done = bf16[4096,512]{1,0:T(8,128)(2,1)} async-done(((bf16[256,512]{1,0:T(8,128)(2,1)}), bf16[4096,512]{1,0:T(8,128)(2,1)}) %all-gather.11.cloned.1.call-update) | async-done | bytes 4194320 | tf_op jit(solution)/shard_map/all_gather | solution.py:36
  114.6 6.4 %copy.37 = bf16[512,4096]{1,0:T(8,128)(2,1)} copy(bf16[512,4096]{0,1:T(8,128)(2,1)} %bitcast.150) | data formatting | bytes 8388608 | tf_op jit(solution)/shard_map/dot_general | solution.py:39
  121.1 3.8 %fusion.25 = f32[32,4,128]{2,0,1:T(8,128)S(1)} fusion(bf16[4,128,4096]{2,1,0:T(8,128)(2,1)} %bitcast.147, bf16[1,32,4096]{2,1,0:T(8,128)(2,1)S(1)} %copy-done.1, f32[4096]{0:T(1024)S(1)} %bitcast.157, f32[32]{0:T(128)S(1)} %add_rsqrt_fusion), kind=kOutput, calls=%fused_computation.40 | convolution fusion | flops 134742016 | bytes 4538496 | tf_op jit(solution)/shard_map/dot_general | solution.py:39
  126.3 39.6 %all-gather.13.cloned.1.call-done = bf16[4096,512]{1,0:T(8,128)(2,1)} async-done(((bf16[256,512]{1,0:T(8,128)(2,1)}), bf16[4096,512]{1,0:T(8,128)(2,1)}) %all-gather.13.cloned.1.call-update) | async-done | bytes 4194320 | tf_op jit(solution)/shard_map/all_gather | solution.py:37
  165.9 3.1 %fusion.7 = bf16[4,4,8,128]{3,2,1,0:T(8,128)(2,1)S(1)} fusion(bf16[4096,512]{1,0:T(8,128)(2,1)} %all-gather.13.cloned.1.call-done, bf16[1,32,4096]{2,1,0:T(8,128)(2,1)S(1)} %copy-done.1, f32[4096]{0:T(1024)S(1)} %bitcast.158, f32[32]{0:T(128)S(1)} %add_rsqrt_fusion), kind=kOutput, calls=%fused_computation.13 | convolution fusion | flops 134758400 | bytes 4505728 | tf_op jit(solution)/shard_map/dot_general | solution.py:40
  169.0 3.4 %all-to-all-start.2 = ((bf16[32,8,128]{2,0,1:T(8,128)(2,1)}), bf16[32,8,128]{2,0,1:T(8,128)(2,1)S(1)}, u32[]{:S(2)}, u32[]{:S(2)}) async-start(bf16[32,8,128]{2,0,1:T(8,128)(2,1)} %copy.38), calls=%async_computation.2 | async-start | bytes 131072 | tf_op jit(solution)/shard_map/all_to_all | solution.py:100
  172.5 6.7 %all-to-all-done.2 = bf16[32,8,128]{2,0,1:T(8,128)(2,1)S(1)} async-done(((bf16[32,8,128]{2,0,1:T(8,128)(2,1)}), bf16[32,8,128]{2,0,1:T(8,128)(2,1)S(1)}, u32[]{:S(2)}, u32[]{:S(2)}) %all-to-all-start.2) | async-done | bytes 65568 | tf_op jit(solution)/shard_map/all_to_all | solution.py:100
  179.9 3.4 %all-to-all-start.5 = ((bf16[32,8,128]{2,0,1:T(8,128)(2,1)}), bf16[32,8,128]{2,0,1:T(8,128)(2,1)S(1)}, u32[]{:S(2)}, u32[]{:S(2)}) async-start(bf16[32,8,128]{2,0,1:T(8,128)(2,1)} %bitcast.37), calls=%async_computation.5 | async-start | bytes 131072 | tf_op jit(solution)/shard_map/all_to_all | solution.py:101
  183.3 34.1 %all-gather.9.cloned.1.call-done = bf16[4096,512]{1,0:T(8,128)(2,1)} async-done(((bf16[256,512]{1,0:T(8,128)(2,1)}), bf16[4096,512]{1,0:T(8,128)(2,1)}) %all-gather.9.cloned.1.call-update) | async-done | bytes 4194320 | tf_op jit(solution)/shard_map/all_gather | solution.py:37
  221.1 3.4 %all-to-all-start.1 = ((bf16[32,8,128]{2,0,1:T(8,128)(2,1)}), bf16[32,8,128]{2,0,1:T(8,128)(2,1)S(1)}, u32[]{:S(2)}, u32[]{:S(2)}) async-start(bf16[32,8,128]{2,0,1:T(8,128)(2,1)} %bitcast.13), calls=%async_computation.1 | async-start | bytes 131072 | tf_op jit(solution)/shard_map/all_to_all | solution.py:101
  224.7 6.6 %all-to-all-done.1 = bf16[32,8,128]{2,0,1:T(8,128)(2,1)S(1)} async-done(((bf16[32,8,128]{2,0,1:T(8,128)(2,1)}), bf16[32,8,128]{2,0,1:T(8,128)(2,1)S(1)}, u32[]{:S(2)}, u32[]{:S(2)}) %all-to-all-start.1) | async-done | bytes 65568 | tf_op jit(solution)/shard_map/all_to_all | solution.py:101
  231.9 3.4 %all-to-all-start.4 = ((bf16[32,8,128]{2,0,1:T(8,128)(2,1)}), bf16[32,8,128]{2,0,1:T(8,128)(2,1)S(1)}, u32[]{:S(2)}, u32[]{:S(2)}) async-start(bf16[32,8,128]{2,0,1:T(8,128)(2,1)} %bitcast.27), calls=%async_computation.4 | async-start | bytes 131072 | tf_op jit(solution)/shard_map/all_to_all | solution.py:102
  235.9 6.3 %all-to-all-done.4 = bf16[32,8,128]{2,0,1:T(8,128)(2,1)S(1)} async-done(((bf16[32,8,128]{2,0,1:T(8,128)(2,1)}), bf16[32,8,128]{2,0,1:T(8,128)(2,1)S(1)}, u32[]{:S(2)}, u32[]{:S(2)}) %all-to-all-start.4) | async-done | bytes 65568 | tf_op jit(solution)/shard_map/all_to_all | solution.py:102
  242.8 3.4 %all-to-all-start = ((bf16[32,8,128]{2,0,1:T(8,128)(2,1)}), bf16[32,8,128]{2,0,1:T(8,128)(2,1)S(1)}, u32[]{:S(2)}, u32[]{:S(2)}) async-start(bf16[32,8,128]{2,0,1:T(8,128)(2,1)} %bitcast.2), calls=%async_computation | async-start | bytes 131072 | tf_op jit(solution)/shard_map/all_to_all | solution.py:102
  248.4 4.6 %all-to-all-done = bf16[32,8,128]{2,0,1:T(8,128)(2,1)S(1)} async-done(((bf16[32,8,128]{2,0,1:T(8,128)(2,1)}), bf16[32,8,128]{2,0,1:T(8,128)(2,1)S(1)}, u32[]{:S(2)}, u32[]{:S(2)}) %all-to-all-start) | async-done | bytes 65568 | tf_op jit(solution)/shard_map/all_to_all | solution.py:102
  253.0 3.3 %all-to-all-start.7 = ((bf16[8,2,2048]{2,1,0:T(2,128)(2,1)}), bf16[8,2,2048]{2,1,0:T(2,128)(2,1)S(1)}, u32[]{:S(2)}, u32[]{:S(2)}) async-start(bf16[8,2,2048]{2,1,0:T(2,128)(2,1)} %reshape.256), calls=%async_computation.7 | async-start | bytes 131072 | tf_op jit(solution)/shard_map/all_to_all | solution.py:105
  258.1 5.1 %all-to-all-done.7 = bf16[8,2,2048]{2,1,0:T(2,128)(2,1)S(1)} async-done(((bf16[8,2,2048]{2,1,0:T(2,128)(2,1)}), bf16[8,2,2048]{2,1,0:T(2,128)(2,1)S(1)}, u32[]{:S(2)}, u32[]{:S(2)}) %all-to-all-start.7) | async-done | bytes 65568 | tf_op jit(solution)/shard_map/all_to_all | solution.py:105
  263.2 3.4 %all-to-all-start.3 = ((bf16[8,2,2048]{2,1,0:T(2,128)(2,1)}), bf16[8,2,2048]{2,1,0:T(2,128)(2,1)S(1)}, u32[]{:S(2)}, u32[]{:S(2)}) async-start(bf16[8,2,2048]{2,1,0:T(2,128)(2,1)} %reshape.254), calls=%async_computation.3 | async-start | bytes 131072 | tf_op jit(solution)/shard_map/all_to_all | solution.py:105
  267.3 6.1 %all-to-all-done.3 = bf16[8,2,2048]{2,1,0:T(2,128)(2,1)S(1)} async-done(((bf16[8,2,2048]{2,1,0:T(2,128)(2,1)}), bf16[8,2,2048]{2,1,0:T(2,128)(2,1)S(1)}, u32[]{:S(2)}, u32[]{:S(2)}) %all-to-all-start.3) | async-done | bytes 65568 | tf_op jit(solution)/shard_map/all_to_all | solution.py:105
  (70 shorter events, 25.8 us)
Async XLA Ops:
  7.2 68.0 %all-gather.15.cloned.1.call-start = ((), (), s32[]{:S(2)}) async-start(), calls=%async_computation.11 | async-start | bytes 4456448 | tf_op jit(solution)/shard_map/all_gather | solution.py:36
  7.9 106.7 %all-gather.11.cloned.1.call-start = ((), (), s32[]{:S(2)}) async-start(), calls=%async_computation.9 | async-start | bytes 4456448 | tf_op jit(solution)/shard_map/all_gather | solution.py:36
  8.6 157.2 %all-gather.13.cloned.1.call-start = ((), (), s32[]{:S(2)}) async-start(), calls=%async_computation.10 | async-start | bytes 4456448 | tf_op jit(solution)/shard_map/all_gather | solution.py:37
  9.4 208.0 %all-gather.9.cloned.1.call-start = ((), (), s32[]{:S(2)}) async-start(), calls=%async_computation.8 | async-start | bytes 4456448 | tf_op jit(solution)/shard_map/all_gather | solution.py:37
  11.5 157.5 %all-to-all-start.6 = ((bf16[32,8,128]{2,0,1:T(8,128)(2,1)}), bf16[32,8,128]{2,0,1:T(8,128)(2,1)S(1)}, u32[]{:S(2)}, u32[]{:S(2)}) async-start(bf16[32,8,128]{2,0,1:T(8,128)(2,1)} %copy.43), calls=%async_computation.6 | async-start | bytes 131072 | tf_op jit(solution)/shard_map/all_to_all | solution.py:100
  114.6 6.4 %copy-start.1 = (bf16[1,32,4096]{2,1,0:T(8,128)(2,1)S(1)}, bf16[1,32,4096]{2,1,0:T(8,128)(2,1)}, u32[]{:S(2)}) copy-start(bf16[1,32,4096]{2,1,0:T(8,128)(2,1)} %param.18) | copy-start | bytes 786436
  121.1 3.8 %copy-start = (bf16[512,4096]{1,0:T(8,128)(2,1)S(1)}, bf16[512,4096]{1,0:T(8,128)(2,1)}, u32[]{:S(2)}) copy-start(bf16[512,4096]{1,0:T(8,128)(2,1)} %copy.37) | copy-start | bytes 12582916
  121.1 3.9 %copy-start.2 = (bf16[1,32,4096]{2,1,0:T(8,128)(2,1)S(1)}, bf16[1,32,4096]{2,1,0:T(8,128)(2,1)}, u32[]{:S(2)}) copy-start(bf16[1,32,4096]{2,1,0:T(8,128)(2,1)} %param.12) | copy-start | bytes 786436
  169.0 10.3 %all-to-all-start.2 = ((bf16[32,8,128]{2,0,1:T(8,128)(2,1)}), bf16[32,8,128]{2,0,1:T(8,128)(2,1)S(1)}, u32[]{:S(2)}, u32[]{:S(2)}) async-start(bf16[32,8,128]{2,0,1:T(8,128)(2,1)} %copy.38), calls=%async_computation.2 | async-start | bytes 131072 | tf_op jit(solution)/shard_map/all_to_all | solution.py:100
  179.9 40.5 %all-to-all-start.5 = ((bf16[32,8,128]{2,0,1:T(8,128)(2,1)}), bf16[32,8,128]{2,0,1:T(8,128)(2,1)S(1)}, u32[]{:S(2)}, u32[]{:S(2)}) async-start(bf16[32,8,128]{2,0,1:T(8,128)(2,1)} %bitcast.37), calls=%async_computation.5 | async-start | bytes 131072 | tf_op jit(solution)/shard_map/all_to_all | solution.py:101
  221.1 10.2 %all-to-all-start.1 = ((bf16[32,8,128]{2,0,1:T(8,128)(2,1)}), bf16[32,8,128]{2,0,1:T(8,128)(2,1)S(1)}, u32[]{:S(2)}, u32[]{:S(2)}) async-start(bf16[32,8,128]{2,0,1:T(8,128)(2,1)} %bitcast.13), calls=%async_computation.1 | async-start | bytes 131072 | tf_op jit(solution)/shard_map/all_to_all | solution.py:101
  231.9 10.2 %all-to-all-start.4 = ((bf16[32,8,128]{2,0,1:T(8,128)(2,1)}), bf16[32,8,128]{2,0,1:T(8,128)(2,1)S(1)}, u32[]{:S(2)}, u32[]{:S(2)}) async-start(bf16[32,8,128]{2,0,1:T(8,128)(2,1)} %bitcast.27), calls=%async_computation.4 | async-start | bytes 131072 | tf_op jit(solution)/shard_map/all_to_all | solution.py:102
  242.8 10.2 %all-to-all-start = ((bf16[32,8,128]{2,0,1:T(8,128)(2,1)}), bf16[32,8,128]{2,0,1:T(8,128)(2,1)S(1)}, u32[]{:S(2)}, u32[]{:S(2)}) async-start(bf16[32,8,128]{2,0,1:T(8,128)(2,1)} %bitcast.2), calls=%async_computation | async-start | bytes 131072 | tf_op jit(solution)/shard_map/all_to_all | solution.py:102
  253.0 10.2 %all-to-all-start.7 = ((bf16[8,2,2048]{2,1,0:T(2,128)(2,1)}), bf16[8,2,2048]{2,1,0:T(2,128)(2,1)S(1)}, u32[]{:S(2)}, u32[]{:S(2)}) async-start(bf16[8,2,2048]{2,1,0:T(2,128)(2,1)} %reshape.256), calls=%async_computation.7 | async-start | bytes 131072 | tf_op jit(solution)/shard_map/all_to_all | solution.py:105
  263.2 10.2 %all-to-all-start.3 = ((bf16[8,2,2048]{2,1,0:T(2,128)(2,1)}), bf16[8,2,2048]{2,1,0:T(2,128)(2,1)S(1)}, u32[]{:S(2)}, u32[]{:S(2)}) async-start(bf16[8,2,2048]{2,1,0:T(2,128)(2,1)} %reshape.254), calls=%async_computation.3 | async-start | bytes 131072 | tf_op jit(solution)/shard_map/all_to_all | solution.py:105
Sparse Core Ops, SparseCore 0:
  10.1 53.3 all-gather.14
  65.7 48.9 all-gather.10
  116.8 49.0 all-gather.12
  167.9 49.4 all-gather.8
where the time goes:
time: 282 us; the launch traced here: 281 us
  waiting for transfers between devices  145 us (51%)
  blocking collectives  47.7 us (17%)
  starting transfers between devices  30.9 us (11%)
  local copies, waits for them, and re-layouts  26 us (9%)
  between operations  14.7 us (5%)
  matrix products  12.5 us (4%)
  other arithmetic  4.27 us (2%)
    all_gather x2, waiting for transfers between devices, project(): lax.all_gather(value_weight, ('sp', 'fsdp'), axis=0, tiled=True)  73.7 us
    all_gather x2, blocking collectives, project(): gain_rows = lax.all_gather(gain, ('sp', 'fsdp'), axis=0, tiled=True)  39.6 us
    all_gather x2, waiting for transfers between devices, project(): key_rows = lax.all_gather(key_weight, ('sp', 'fsdp'), axis=0, tiled=True)  33.1 us
    dot_general x2, local copies, waits for them, and re-layouts, project(): raw_keys = jnp.dot(normed, key_rows, preferred_element_type=jnp.float32)  12.8 us
    all_to_all x2, waiting for transfers between devices, run_model(): lax.all_to_all(mixed, 'sp', split_axis=0, concat_axis=1, tiled=True)  11.1 us
    all_to_all x2, waiting for transfers between devices, run_model(): lax.all_to_all(wide_values, 'sp', split_axis=1, concat_axis=0, tiled=True)  10.8 us
    all_to_all x2, starting transfers between devices, run_model(): lax.all_to_all(query_local, 'sp', split_axis=1, concat_axis=0, tiled=True)  10.7 us
    all_gather x1, blocking collectives, run_model(): every_doc = lax.all_gather(documents[0], 'sp', axis=0, tiled=True)  8.09 us
  transfers between devices with their start and end apart: 12, of which 9 were waited for; matrix products, arithmetic and copies ran while one was open for 14% of the time, Pallas kernels for 0%

commit v1 on v0

--- a/solution.py
+++ b/solution.py
@@ -1,6 +1,10 @@
+import functools
+
 import jax
 import jax.numpy as jnp
 from jax import lax
+from jax.experimental import pallas as pl
+from jax.experimental.pallas import tpu as pltpu
 from jax.sharding import PartitionSpec as P
 
 HEAD_DIM = 128
@@ -9,6 +13,8 @@
 EPS = 1e-05
 ROPE_BASE = 500000.0
 MASKED = -1e30
+LANES = 128
+GAIN_ROWS = 16
 
 
 def rotate(raw_keys, positions):
@@ -106,42 +112,237 @@
     return returned.reshape(1, tokens, head_count * HEAD_DIM)
 
 
-def per_device(
-    policy_hidden,
-    policy_queries,
-    policy_documents,
-    policy_gain,
-    policy_key_weight,
-    policy_value_weight,
-    frozen_hidden,
-    frozen_queries,
-    frozen_documents,
-    frozen_gain,
-    frozen_key_weight,
-    frozen_value_weight,
-):
-    policy_mixed = run_model(
-        policy_hidden,
-        policy_queries,
-        policy_documents,
-        policy_gain,
-        policy_key_weight,
-        policy_value_weight,
-    )
-    frozen_mixed = run_model(
-        frozen_hidden,
-        frozen_queries,
-        frozen_documents,
-        frozen_gain,
-        frozen_key_weight,
-        frozen_value_weight,
-    )
-    return (policy_mixed, frozen_mixed)
+def gathered_weights(policy, frozen):
+    return (run_model(*policy), run_model(*frozen))
+
+
+def pack_kernel(hidden_p, hidden_f, queries_p, queries_f, docs_p, docs_f, out):
+    planes, _, tokens, _ = out.shape
+    features = hidden_p.shape[1] // planes
+    per_head = queries_p.shape[1] // planes
+    lane = lax.broadcasted_iota(jnp.int32, (tokens, LANES), 1)
+    diagonal = lax.broadcasted_iota(jnp.int32, (tokens, tokens), 0) == lax.broadcasted_iota(
+        jnp.int32, (tokens, tokens), 1
+    )
+    for model, (hidden, queries, docs) in enumerate(
+        ((hidden_p, queries_p, docs_p), (hidden_f, queries_f, docs_f))
+    ):
+        widened = hidden[...].astype(jnp.float32)
+        mean = jnp.sum(widened * widened, axis=-1, keepdims=True) * (1.0 / hidden.shape[1])
+        inverse = lax.rsqrt(mean + EPS)
+        high = inverse.astype(jnp.bfloat16).astype(jnp.float32)
+        middle = (inverse - high).astype(jnp.bfloat16).astype(jnp.float32)
+        low = inverse - high - middle
+        doc = jnp.sum(
+            jnp.where(diagonal, docs[...].astype(jnp.float32), 0.0), axis=-1, keepdims=True
+        )
+        side = jnp.where(lane == 0, high, 0.0)
+        side = jnp.where(lane == 1, middle, side)
+        side = jnp.where(lane == 2, low, side)
+        side = jnp.where(lane == 3, doc, side).astype(jnp.bfloat16)
+        for plane in range(planes):
+            out[plane, model, :, :features] = hidden[:, plane * features : (plane + 1) * features]
+            out[plane, model, :, features : features + per_head] = queries[
+                :, plane * per_head : (plane + 1) * per_head
+            ]
+            out[plane, model, :, features + per_head :] = side
+
+
+def weights_kernel(model_ref, gain_p, key_p, value_p, gain_f, key_f, value_f, keep, send):
+    rows, width = key_p.shape
+
+    def fill(out, gain, key, value):
+        out[:rows, :width] = key[...]
+        out[:rows, width:] = value[...]
+        out[rows:, :rows] = jnp.broadcast_to(gain[...], (GAIN_ROWS, rows))
+
+    @pl.when(model_ref[0] == 0)
+    def _():
+        fill(keep, gain_p, key_p, value_p)
+        fill(send, gain_f, key_f, value_f)
+
+    @pl.when(model_ref[0] != 0)
+    def _():
+        fill(keep, gain_f, key_f, value_f)
+        fill(send, gain_p, key_p, value_p)
+
+
+def partial_kernel(place_ref, packed, own_keep, own_got, pair_keep, pair_got, *outs_and_scratch):
+    outs, keys, values = outs_and_scratch[:-2], outs_and_scratch[-2], outs_and_scratch[-1]
+    plane, model, core = place_ref[0], place_ref[1], place_ref[2]
+    planes = len(outs)
+    senders, tokens, _ = packed.shape
+    length = senders * tokens
+    rows = own_keep.shape[0] - GAIN_ROWS
+    width = own_keep.shape[1] // 2
+    features = 4 * rows
+    side = packed[:, :, packed.shape[2] - LANES :].reshape(length, LANES).astype(jnp.float32)
+    inverse = side[:, 0:1] + side[:, 1:2] + side[:, 2:3]
+    key_sum = value_sum = None
+    for flip_core, flip_model, block in (
+        (0, 0, own_keep),
+        (0, 1, own_got),
+        (1, 0, pair_keep),
+        (1, 1, pair_got),
+    ):
+        first = pl.multiple_of(((model ^ flip_model) * 2 + (core ^ flip_core)) * rows, rows)
+        hidden = packed[:, :, pl.ds(first, rows)].reshape(length, rows).astype(jnp.float32)
+        gain = block[rows : rows + 1, :rows].astype(jnp.float32)
+        normed = (hidden * inverse * gain).astype(jnp.bfloat16)
+        key_part = jnp.dot(normed, block[:rows, :width], preferred_element_type=jnp.float32)
+        value_part = jnp.dot(normed, block[:rows, width:], preferred_element_type=jnp.float32)
+        key_sum = key_part if key_sum is None else key_sum + key_part
+        value_sum = value_part if value_sum is None else value_sum + value_part
+    for head in range(planes):
+        keys[head] = key_sum[:, head * HEAD_DIM : (head + 1) * HEAD_DIM]
+        values[head] = value_sum[:, head * HEAD_DIM : (head + 1) * HEAD_DIM]
+    for flip in range(planes):
+        outs[flip][:, :HEAD_DIM] = keys[plane ^ flip]
+        outs[flip][:, HEAD_DIM:] = values[plane ^ flip]
+
+
+def attend_kernel(packed, cosines, sines, *parts_and_out):
+    parts, out = parts_and_out[:-1], parts_and_out[-1]
+    senders, tokens, wide = packed.shape
+    length = senders * tokens
+    per_head = out.shape[2]
+    total = parts[0][...]
+    for part in parts[1:]:
+        total = total + part[...]
+    raw_keys = total[:, :HEAD_DIM]
+    turned = jnp.concatenate(
+        [raw_keys[:, HEAD_DIM // 2 :], raw_keys[:, : HEAD_DIM // 2]], axis=-1
+    )
+    keys = (raw_keys * cosines[...] + turned * sines[...]).astype(jnp.bfloat16)
+    values = total[:, HEAD_DIM:].astype(jnp.bfloat16)
+    side = packed[:, :, wide - LANES :].reshape(length, LANES).astype(jnp.float32)
+    query_docs = side[:, 3:4]
+    key_docs = jnp.transpose(side)[3:4, :]
+    row = lax.broadcasted_iota(jnp.int32, (length, length), 0)
+    column = lax.broadcasted_iota(jnp.int32, (length, length), 1)
+    allowed = (column <= row) & (query_docs == key_docs)
+    for head in range(per_head // HEAD_DIM):
+        first = wide - LANES - per_head + head * HEAD_DIM
+        queries = packed[:, :, first : first + HEAD_DIM].reshape(length, HEAD_DIM)
+        scores = lax.dot_general(
+            queries, keys, (((1,), (1,)), ((), ())), preferred_element_type=jnp.float32
+        ) * (HEAD_DIM ** (-0.5))
+        scores = jnp.where(allowed, scores, MASKED)
+        highest = jnp.max(scores, axis=-1, keepdims=True)
+        exponent = jnp.where(allowed, jnp.exp(scores - highest), 0.0)
+        weights = (exponent / jnp.sum(exponent, axis=-1, keepdims=True)).astype(jnp.bfloat16)
+        mixed = jnp.dot(weights, values, preferred_element_type=jnp.float32)
+        out[:, :, head * HEAD_DIM : (head + 1) * HEAD_DIM] = mixed.astype(jnp.bfloat16).reshape(
+            senders, tokens, HEAD_DIM
+        )
+
+
+def rotary_tables(length):
+    half_dim = HEAD_DIM // 2
+    frequency = jnp.exp(
+        -jnp.log(ROPE_BASE) * jnp.arange(half_dim, dtype=jnp.float32) * 2.0 / HEAD_DIM
+    )
+    angles = jnp.arange(length, dtype=jnp.int32).astype(jnp.float32)[:, None] * frequency[None, :]
+    cosines, sines = jnp.cos(angles), jnp.sin(angles)
+    return (
+        jnp.concatenate([cosines, cosines], axis=-1),
+        jnp.concatenate([-sines, sines], axis=-1),
+    )
+
+
+def planes_contract(planes, policy, frozen):
+    hidden_p, queries_p, docs_p, gain_p, key_p, value_p = policy
+    hidden_f, queries_f, docs_f, gain_f, key_f, value_f = frozen
+    tokens, depth = hidden_p.shape[1:]
+    rows, width = key_p.shape
+    per_head = queries_p.shape[2] // planes
+    wide = depth // planes + per_head + LANES
+    senders = 2 * planes
+    length = senders * tokens
+    place = lax.axis_index("sp")
+    core = lax.axis_index("fsdp")
+    plane, model = place // 2, place % 2
+    vmem = pl.BlockSpec(memory_space=pltpu.VMEM)
+    smem = pl.BlockSpec(memory_space=pltpu.SMEM)
+
+    across = [(i, i ^ 1) for i in range(senders)]
+    swap = [(0, 1), (1, 0)]
+    keep, send = pl.pallas_call(
+        weights_kernel,
+        out_shape=[jax.ShapeDtypeStruct((rows + GAIN_ROWS, 2 * width), jnp.bfloat16)] * 2,
+        in_specs=[smem] + [vmem] * 6,
+        out_specs=[vmem] * 2,
+        name="weights",
+    )(
+        model.reshape(1),
+        gain_p.reshape(1, rows),
+        key_p,
+        value_p,
+        gain_f.reshape(1, rows),
+        key_f,
+        value_f,
+    )
+    got = lax.ppermute(send, "sp", across)
+    packed = pl.pallas_call(
+        pack_kernel,
+        out_shape=jax.ShapeDtypeStruct((planes, 2, tokens, wide), jnp.bfloat16),
+        in_specs=[vmem] * 6,
+        out_specs=vmem,
+        name="pack",
+    )(hidden_p[0], hidden_f[0], queries_p[0], queries_f[0], docs_p, docs_f)
+    packed = lax.all_to_all(
+        packed.reshape(senders, tokens, wide), "sp", split_axis=0, concat_axis=0, tiled=True
+    )
+    pair_keep = lax.ppermute(keep, "fsdp", swap)
+    pair_got = lax.ppermute(got, "fsdp", swap)
+    part_shape = jax.ShapeDtypeStruct((length, 2 * HEAD_DIM), jnp.float32)
+    parts = pl.pallas_call(
+        partial_kernel,
+        out_shape=[part_shape] * planes,
+        in_specs=[smem] + [vmem] * 5,
+        out_specs=[vmem] * planes,
+        scratch_shapes=[pltpu.VMEM((planes, length, HEAD_DIM), jnp.float32)] * 2,
+        name="partial",
+    )(jnp.stack([plane, model, core]), packed, keep, got, pair_keep, pair_got)
+    arrived = [parts[0]] + [
+        lax.ppermute(parts[flip], "sp", [(i, i ^ (2 * flip)) for i in range(senders)])
+        for flip in range(1, planes)
+    ]
+    cosines, sines = rotary_tables(length)
+    mixed = pl.pallas_call(
+        attend_kernel,
+        out_shape=jax.ShapeDtypeStruct((senders, tokens, per_head), jnp.bfloat16),
+        in_specs=[vmem] * (3 + planes),
+        out_specs=vmem,
+        name="attend",
+    )(packed, cosines, sines, *arrived)
+    mixed = lax.all_to_all(mixed, "sp", split_axis=0, concat_axis=0, tiled=True)
+    mixed = mixed.reshape(planes, 2, tokens, per_head).transpose(1, 2, 0, 3)
+    mixed = mixed.reshape(2, 1, tokens, planes * per_head)
+    return (mixed[0], mixed[1])
+
+
+def per_device(sp_size, fsdp_size, *arrays):
+    policy, frozen = arrays[:6], arrays[6:]
+    key_heads = policy[4].shape[1] // HEAD_DIM
+    tokens, depth = policy[0].shape[1:]
+    planes = sp_size // 2
+    if (
+        sp_size == 2 * key_heads
+        and planes & (planes - 1) == 0
+        and fsdp_size == 2
+        and tokens % 16 == 0
+        and policy[4].shape[0] % LANES == 0
+        and 2 * policy[4].shape[0] <= 2 * policy[4].shape[1]
+        and sp_size * tokens <= 512
+    ):
+        return planes_contract(planes, policy, frozen)
+    return gathered_weights(policy, frozen)
 
 
 def solution(mesh):
     return jax.shard_map(
-        per_device,
+        functools.partial(per_device, mesh.shape["sp"], mesh.shape["fsdp"]),
         mesh=mesh,
         in_specs=(
             P(("groups", "fsdp"), "sp", None),

time: 282 us -> 83.3 us (0.30)
  waiting for transfers between devices: 145 us -> 35.2 us
  blocking collectives: 47.7 us -> 14.3 us
  local copies, waits for them, and re-layouts: 26 us -> 5.64 us
  starting transfers between devices: 30.9 us -> 13.7 us
  between operations: 14.7 us -> 0.68 us
  matrix products: 12.5 us -> 0 us
  Pallas kernels: 0 us -> 11.3 us
    all_gather x4 -> x0, waiting for transfers between devices: 107 us -> none  [the longest x2 73.7 us: project(): lax.all_gather(value_weight, ('sp', 'fsdp'), axis=0, tiled=True)]
    all_gather x3 -> x0, blocking collectives: 47.7 us -> none  [the longest x2 39.6 us: project(): gain_rows = lax.all_gather(gain, ('sp', 'fsdp'), axis=0, tiled=True)]
    all_to_all x8 -> x1, waiting for transfers between devices: 35.3 us -> 0.01 us  [planes_contract(): lax.all_to_all(packed.reshape(senders, tokens, wide), 'sp', split_axis=0,...]
    ppermute x0 -> x6, waiting for transfers between devices: none -> 35.2 us  [the longest x3 17.7 us: planes_contract(): lax.ppermute(parts[flip], 'sp', [(i, i ^ 2 * flip) for i in range(senders)])]
    all_to_all x8 -> x1, starting transfers between devices: 30.8 us -> 7.31 us  [planes_contract(): lax.all_to_all(packed.reshape(senders, tokens, wide), 'sp', split_axis=0,...]
    all_to_all x0 -> x1, blocking collectives: none -> 14.3 us  [planes_contract(): mixed = lax.all_to_all(mixed, 'sp', split_axis=0, concat_axis=0, tiled=True)]
    dot_general x2 -> x0, local copies, waits for them, and re-layouts: 12.8 us -> none  [project(): raw_keys = jnp.dot(normed, key_rows, preferred_element_type=jnp.float32)]
    dot_general x8 -> x0, matrix products: 12.5 us -> none  [the longest x2 6.11 us: project(): raw_values = jnp.dot(normed, value_rows, preferred_element_type=jnp.float32)]
  transfers between devices with their start and end apart: 12 -> 7, of which waited for: 9 -> 4; matrix products, arithmetic and copies ran while one was open for 14% -> 4% of each run, Pallas kernels for 0% -> 3%
where the time goes in v1:
time: 83.3 us; the launch traced here: 82.9 us
  waiting for transfers between devices  35.2 us (42%)
  blocking collectives  14.3 us (17%)
  starting transfers between devices  13.7 us (16%)
  Pallas kernels  11.3 us (14%)
  local copies, waits for them, and re-layouts  5.64 us (7%)
  other arithmetic  2.06 us (2%)
    ppermute x3, waiting for transfers between devices, planes_contract(): lax.ppermute(parts[flip], 'sp', [(i, i ^ 2 * flip) for i in range(senders)])  17.7 us
    ppermute x1, waiting for transfers between devices, planes_contract(): got = lax.ppermute(send, 'sp', across)  16.3 us
    all_to_all x1, blocking collectives, planes_contract(): mixed = lax.all_to_all(mixed, 'sp', split_axis=0, concat_axis=0, tiled=True)  14.3 us
    all_to_all x1, starting transfers between devices, planes_contract(): lax.all_to_all(packed.reshape(senders, tokens, wide), 'sp', split_axis=0,...  7.31 us
    ppermute x3, starting transfers between devices, planes_contract(): lax.ppermute(parts[flip], 'sp', [(i, i ^ 2 * flip) for i in range(senders)])  4.39 us
    pallas_call x1, Pallas kernels, planes_contract(): pl.pallas_call(partial_kernel, out_shape=[part_shape] * planes, in_specs=...  3.65 us
    unnamed x19, local copies, waits for them, and re-layouts  3.24 us
    pallas_call x1, Pallas kernels, planes_contract(): pl.pallas_call(attend_kernel, out_shape=jax.ShapeDtypeStruct((senders, to...  3.18 us
  transfers between devices with their start and end apart: 7, of which 4 were waited for; matrix products, arithmetic and copies ran while one was open for 4% of the time, Pallas kernels for 3%

profile of v1, /device:TPU:0, one launch (start us, length us, event | category | flops | bytes accessed | tf_op | source)
XLA Modules:
  0.0 82.9 jit_solution(17570928013841979692)
XLA Ops:
  0.6 2.2 %pack.1 = bf16[4,2,32,1408]{3,2,1,0:T(8,128)(2,1)} custom-call(bf16[32,4096]{1,0:T(8,128)(2,1)} %bitcast.19, bf16[32,4096]{1,0:T(8,128)(2,1)} %bitcast.20, bf16[32,1024]{1,0:T(8,128)(2,1)} %bitcast.21, bf16[32,1024]{1,0:T(8,128)(2,1)} %bitcast.22, s32[1,32]{1,0:T(1,128)} %docs_p.1, s32[1,32]{1,0:T(1,128)} %docs_f.1), custom_call_target="tpu_custom_call" | custom-call | tf_op jit(solution)/shard_map/pack/pallas_call | solution.py:286
  2.8 7.3 %all-to-all-start = ((bf16[8,32,1408]{2,1,0:T(8,128)(2,1)}), bf16[8,32,1408]{2,1,0:T(8,128)(2,1)S(1)}, u32[]{:S(2)}, u32[]{:S(2)}) async-start(bf16[8,32,1408]{2,1,0:T(8,128)(2,1)} %bitcast.17), calls=%async_computation | async-start | bytes 1441792 | tf_op jit(solution)/shard_map/all_to_all | solution.py:293
  10.1 0.7 copy-done.7
  10.8 0.6 reshape.32.gain_p
  11.4 0.6 reshape.33.gain_f
  12.0 2.3 %weights.1 = (bf16[272,1024]{1,0:T(8,128)(2,1)}, bf16[272,1024]{1,0:T(8,128)(2,1)}) custom-call(s32[1]{0:T(128)} %bitcast.6.model_ref, bf16[1,256]{1,0:T(2,128)(2,1)} %reshape.32.gain_p, bf16[256,512]{1,0:T(8,128)(2,1)} %key_p.1, bf16[256,512]{1,0:T(8,128)(2,1)} %value_p.1, bf16[1,256]{1,0:T(2,128)(2,1)} %reshape.33.gain_f, bf16[256,512]{1,0:T(8,128)(2,1)} %key_f.1, ...), custom_call_target="tpu_custom_call" | custom-call | tf_op jit(solution)/shard_map/weights/pallas_call | solution.py:270
  14.3 2.0 %collective-permute-start = (bf16[272,1024]{1,0:T(8,128)(2,1)}, bf16[272,1024]{1,0:T(8,128)(2,1)S(1)}, u32[]{:S(2)}, u32[]{:S(2)}) collective-permute-start(bf16[272,1024]{1,0:T(8,128)(2,1)} %get-tuple-element.9), channel_id=1, source_target_pairs={{0,2},{2,0},{4,6},{6,4},{8,10},{10,8},{12,14},{14,12},{1,3},{3,1},... | collective-permute-start | bytes 1671176 | tf_op jit(solution)/shard_map/ppermute | solution.py:285
  16.3 16.3 %collective-permute-done.own_got = bf16[272,1024]{1,0:T(8,128)(2,1)S(1)} collective-permute-done((bf16[272,1024]{1,0:T(8,128)(2,1)}, bf16[272,1024]{1,0:T(8,128)(2,1)S(1)}, u32[]{:S(2)}, u32[]{:S(2)}) %collective-permute-start) | collective-permute-done | bytes 557088 | tf_op jit(solution)/shard_map/ppermute | solution.py:285
  32.6 0.7 pad_add_fusion.place_ref
  33.3 1.3 %collective-permute-done.2.pair_got = bf16[272,1024]{1,0:T(8,128)(2,1)S(1)} collective-permute-done((bf16[272,1024]{1,0:T(8,128)(2,1)S(1)}, bf16[272,1024]{1,0:T(8,128)(2,1)S(1)}, u32[]{:S(2)}, u32[]{:S(2)}) %collective-permute-start.2) | collective-permute-done | bytes 557088 | tf_op jit(solution)/shard_map/ppermute | solution.py:297
  34.6 0.8 copy-done.3
  35.4 0.9 %copy-done = bf16[8,32,1408]{2,1,0:T(8,128)(2,1)} copy-done((bf16[8,32,1408]{2,1,0:T(8,128)(2,1)}, bf16[8,32,1408]{2,1,0:T(8,128)(2,1)S(1)}, u32[]{:S(2)}) %copy-start) | copy-done | bytes 720920
  36.3 3.7 %partial.1 = (f32[256,256]{1,0:T(8,128)}, f32[256,256]{1,0:T(8,128)}, f32[256,256]{1,0:T(8,128)}, f32[256,256]{1,0:T(8,128)}) custom-call(s32[3]{0:T(128)} %pad_add_fusion.place_ref, bf16[8,32,1408]{2,1,0:T(8,128)(2,1)} %copy-done, bf16[272,1024]{1,0:T(8,128)(2,1)} %get-tuple-element.8.own_keep, bf16[272,1024]{1,0:T(8,128)(2,1)} %copy-done.1, ...), custom_call_target="tpu_custom_call" | custom-call | tf_op jit(solution)/shard_map/partial/pallas_call | solution.py:299
  39.9 1.9 %collective-permute-start.3 = (f32[256,256]{1,0:T(8,128)}, f32[256,256]{1,0:T(8,128)S(1)}, u32[]{:S(2)}, u32[]{:S(2)}) collective-permute-start(f32[256,256]{1,0:T(8,128)} %get-tuple-element.11), channel_id=1, source_target_pairs={{0,4},{2,6},{4,0},{6,2},{8,12},{10,14},{12,8},{14,10},{1,5},{3,7},... | collective-permute-start | bytes 786440 | tf_op jit(solution)/shard_map/ppermute | solution.py:308
  41.8 2.4 %collective-permute-start.4 = (f32[256,256]{1,0:T(8,128)}, f32[256,256]{1,0:T(8,128)S(1)}, u32[]{:S(2)}, u32[]{:S(2)}) collective-permute-start(f32[256,256]{1,0:T(8,128)} %get-tuple-element.12), channel_id=1, source_target_pairs={{0,8},{2,10},{4,12},{6,14},{8,0},{10,2},{12,4},{14,6},{1,9},{3,11}... | collective-permute-start | bytes 786440 | tf_op jit(solution)/shard_map/ppermute | solution.py:308
  44.3 0.5 fusion
  44.9 0.8 %pad_maximum_fusion = (f32[256,128]{1,0:T(8,128)}, f32[256,128]{1,0:T(8,128)}) fusion(f32[256,64]{1,0:T(8,128)S(1)} %get-tuple-element.18, f32[256,64]{1,0:T(8,128)S(1)} %get-tuple-element.17, f32[256,64]{1,0:T(8,128)S(1)} %get-tuple-element.16), kind=kLoop, calls=%fused_computation.2 | loop fusion | flops 65536 | bytes 458752 | tf_op jit(solution)/shard_map/concatenate | solution.py:248
  45.7 7.8 %collective-permute-done.3.parts_and_out_1_ = f32[256,256]{1,0:T(8,128)S(1)} collective-permute-done((f32[256,256]{1,0:T(8,128)}, f32[256,256]{1,0:T(8,128)S(1)}, u32[]{:S(2)}, u32[]{:S(2)}) %collective-permute-start.3) | collective-permute-done | bytes 262176 | tf_op jit(solution)/shard_map/ppermute | solution.py:308
  53.5 9.9 %collective-permute-done.4.parts_and_out_2_ = f32[256,256]{1,0:T(8,128)S(1)} collective-permute-done((f32[256,256]{1,0:T(8,128)}, f32[256,256]{1,0:T(8,128)S(1)}, u32[]{:S(2)}, u32[]{:S(2)}) %collective-permute-start.4) | collective-permute-done | bytes 262176 | tf_op jit(solution)/shard_map/ppermute | solution.py:308
  63.4 0.7 copy-done.5
  64.2 3.2 %attend.1 = bf16[8,32,256]{2,1,0:T(8,128)(2,1)} custom-call(bf16[8,32,1408]{2,1,0:T(8,128)(2,1)} %copy-done, f32[256,128]{1,0:T(8,128)} %get-tuple-element.19.cosines, f32[256,128]{1,0:T(8,128)} %get-tuple-element.20.sines, f32[256,256]{1,0:T(8,128)} %get-tuple-element.10.parts_and_out_0_, f32[256,256]{1,0:T(8,128)} %copy-done.4, f32[256,256]{1,0:T(8,128)} %copy-done.5, ...), custom_call_target="tpu_custom_call" | custom-call | tf_op jit(solution)/shard_map/attend/pallas_call | solution.py:312
  67.4 14.3 %all_to_all.10 = bf16[8,32,256]{2,1,0:T(8,128)(2,1)S(1)} all-to-all(bf16[8,32,256]{2,1,0:T(8,128)(2,1)} %attend.1), channel_id=1, replica_groups=mesh['groups'=2,'sp'=8,'fsdp'=2] {'sp'}, dimensions={0} | all-to-all | bytes 262144 | tf_op jit(solution)/shard_map/all_to_all | solution.py:319
  81.6 0.6 copy.16
  82.3 0.6 copy.17
  (23 shorter events, 0.3 us)
Async XLA Ops:
  2.8 31.8 %all-to-all-start = ((bf16[8,32,1408]{2,1,0:T(8,128)(2,1)}), bf16[8,32,1408]{2,1,0:T(8,128)(2,1)S(1)}, u32[]{:S(2)}, u32[]{:S(2)}) async-start(bf16[8,32,1408]{2,1,0:T(8,128)(2,1)} %bitcast.17), calls=%async_computation | async-start | bytes 1441792 | tf_op jit(solution)/shard_map/all_to_all | solution.py:293
  10.1 0.7 copy-start.7
  10.8 0.7 copy-start.8
  14.3 18.3 %collective-permute-start = (bf16[272,1024]{1,0:T(8,128)(2,1)}, bf16[272,1024]{1,0:T(8,128)(2,1)S(1)}, u32[]{:S(2)}, u32[]{:S(2)}) collective-permute-start(bf16[272,1024]{1,0:T(8,128)(2,1)} %get-tuple-element.9), channel_id=1, source_target_pairs={{0,2},{2,0},{4,6},{6,4},{8,10},{10,8},{12,14},{14,12},{1,3},{3,1},... | collective-permute-start | bytes 1671176 | tf_op jit(solution)/shard_map/ppermute | solution.py:285
  16.3 17.0 %collective-permute-start.1 = (bf16[272,1024]{1,0:T(8,128)(2,1)}, bf16[272,1024]{1,0:T(8,128)(2,1)S(1)}, u32[]{:S(2)}, u32[]{:S(2)}) collective-permute-start(bf16[272,1024]{1,0:T(8,128)(2,1)} %get-tuple-element.8.own_keep), channel_id=1, source_target_pairs={{0,1},{1,0},{2,3},{3,2},{4,5},{5,4},{6,7},{7,6},{8,9},{9,8},{10,11... | collective-permute-start | bytes 1671176 | tf_op jit(solution)/shard_map/ppermute | solution.py:296
  32.6 2.0 %copy-start.1 = (bf16[272,1024]{1,0:T(8,128)(2,1)}, bf16[272,1024]{1,0:T(8,128)(2,1)S(1)}, u32[]{:S(2)}) copy-start(bf16[272,1024]{1,0:T(8,128)(2,1)S(1)} %collective-permute-done.own_got) | copy-start | bytes 1671172
  32.6 2.0 %collective-permute-start.2 = (bf16[272,1024]{1,0:T(8,128)(2,1)S(1)}, bf16[272,1024]{1,0:T(8,128)(2,1)S(1)}, u32[]{:S(2)}, u32[]{:S(2)}) collective-permute-start(bf16[272,1024]{1,0:T(8,128)(2,1)S(1)} %collective-permute-done.own_got), channel_id=1, source_target_pairs={{0,1},{1,0},{2,3},{3,2},{4,5},{5,4},{6,7},{7,6},{8,9},{9,8},{10,11... | collective-permute-start | bytes 1671176 | tf_op jit(solution)/shard_map/ppermute | solution.py:297
  33.3 1.3 %copy-start.2 = (bf16[272,1024]{1,0:T(8,128)(2,1)}, bf16[272,1024]{1,0:T(8,128)(2,1)S(1)}, u32[]{:S(2)}) copy-start(bf16[272,1024]{1,0:T(8,128)(2,1)S(1)} %collective-permute-done.1.pair_keep) | copy-start | bytes 1671172
  34.6 0.8 copy-start.3
  35.4 0.9 %copy-start = (bf16[8,32,1408]{2,1,0:T(8,128)(2,1)}, bf16[8,32,1408]{2,1,0:T(8,128)(2,1)S(1)}, u32[]{:S(2)}) copy-start(bf16[8,32,1408]{2,1,0:T(8,128)(2,1)S(1)} %all-to-all-done.packed) | copy-start | bytes 2162692
  39.9 13.6 %collective-permute-start.3 = (f32[256,256]{1,0:T(8,128)}, f32[256,256]{1,0:T(8,128)S(1)}, u32[]{:S(2)}, u32[]{:S(2)}) collective-permute-start(f32[256,256]{1,0:T(8,128)} %get-tuple-element.11), channel_id=1, source_target_pairs={{0,4},{2,6},{4,0},{6,2},{8,12},{10,14},{12,8},{14,10},{1,5},{3,7},... | collective-permute-start | bytes 786440 | tf_op jit(solution)/shard_map/ppermute | solution.py:308
  41.8 21.5 %collective-permute-start.4 = (f32[256,256]{1,0:T(8,128)}, f32[256,256]{1,0:T(8,128)S(1)}, u32[]{:S(2)}, u32[]{:S(2)}) collective-permute-start(f32[256,256]{1,0:T(8,128)} %get-tuple-element.12), channel_id=1, source_target_pairs={{0,8},{2,10},{4,12},{6,14},{8,0},{10,2},{12,4},{14,6},{1,9},{3,11}... | collective-permute-start | bytes 786440 | tf_op jit(solution)/shard_map/ppermute | solution.py:308
  44.2 19.1 %collective-permute-start.5 = (f32[256,256]{1,0:T(8,128)}, f32[256,256]{1,0:T(8,128)S(1)}, u32[]{:S(2)}, u32[]{:S(2)}) collective-permute-start(f32[256,256]{1,0:T(8,128)} %get-tuple-element.13), channel_id=1, source_target_pairs={{0,12},{2,14},{4,8},{6,10},{8,4},{10,6},{12,0},{14,2},{1,13},{3,15... | collective-permute-start | bytes 786440 | tf_op jit(solution)/shard_map/ppermute | solution.py:308
  53.5 9.9 %copy-start.4 = (f32[256,256]{1,0:T(8,128)}, f32[256,256]{1,0:T(8,128)S(1)}, u32[]{:S(2)}) copy-start(f32[256,256]{1,0:T(8,128)S(1)} %collective-permute-done.3.parts_and_out_1_) | copy-start | bytes 786436
  63.4 0.7 copy-start.5
  63.4 0.8 copy-start.6

commit v2 on v1

--- a/solution.py
+++ b/solution.py
@@ -7,6 +7,7 @@
 from jax.experimental.pallas import tpu as pltpu
 from jax.sharding import PartitionSpec as P
 
+
 HEAD_DIM = 128
 
 
@@ -15,6 +16,7 @@
 MASKED = -1e30
 LANES = 128
 GAIN_ROWS = 16
+KERNEL_BYTES = 16 * 2**20
 
 
 def rotate(raw_keys, positions):
@@ -116,7 +118,42 @@
     return (run_model(*policy), run_model(*frozen))
 
 
-def pack_kernel(hidden_p, hidden_f, queries_p, queries_f, docs_p, docs_f, out):
+def pack_kernel(
+    gain_p,
+    key_p,
+    value_p,
+    gain_f,
+    key_f,
+    value_f,
+    hidden_p,
+    hidden_f,
+    queries_p,
+    queries_f,
+    docs_p,
+    docs_f,
+    send,
+    keep,
+    out,
+):
+    rows, width = key_p.shape
+
+    def fill(target, gain, key, value):
+        target[:rows, :width] = key[...]
+        target[:rows, width:] = value[...]
+        target[rows:, :rows] = jnp.broadcast_to(gain[...].reshape(1, rows), (GAIN_ROWS, rows))
+
+    model = lax.axis_index("sp") % 2
+
+    @pl.when(model == 0)
+    def _():
+        fill(send, gain_f, key_f, value_f)
+        fill(keep, gain_p, key_p, value_p)
+
+    @pl.when(model != 0)
+    def _():
+        fill(send, gain_p, key_p, value_p)
+        fill(keep, gain_f, key_f, value_f)
+
     planes, _, tokens, _ = out.shape
     features = hidden_p.shape[1] // planes
     per_head = queries_p.shape[1] // planes
@@ -124,7 +161,7 @@
     diagonal = lax.broadcasted_iota(jnp.int32, (tokens, tokens), 0) == lax.broadcasted_iota(
         jnp.int32, (tokens, tokens), 1
     )
-    for model, (hidden, queries, docs) in enumerate(
+    for owner, (hidden, queries, docs) in enumerate(
         ((hidden_p, queries_p, docs_p), (hidden_f, queries_f, docs_f))
     ):
         widened = hidden[...].astype(jnp.float32)
@@ -141,41 +178,22 @@
         side = jnp.where(lane == 2, low, side)
         side = jnp.where(lane == 3, doc, side).astype(jnp.bfloat16)
         for plane in range(planes):
-            out[plane, model, :, :features] = hidden[:, plane * features : (plane + 1) * features]
-            out[plane, model, :, features : features + per_head] = queries[
+            out[plane, owner, :, :features] = hidden[:, plane * features : (plane + 1) * features]
+            out[plane, owner, :, features : features + per_head] = queries[
                 :, plane * per_head : (plane + 1) * per_head
             ]
-            out[plane, model, :, features + per_head :] = side
-
-
-def weights_kernel(model_ref, gain_p, key_p, value_p, gain_f, key_f, value_f, keep, send):
-    rows, width = key_p.shape
-
-    def fill(out, gain, key, value):
-        out[:rows, :width] = key[...]
-        out[:rows, width:] = value[...]
-        out[rows:, :rows] = jnp.broadcast_to(gain[...], (GAIN_ROWS, rows))
-
-    @pl.when(model_ref[0] == 0)
-    def _():
-        fill(keep, gain_p, key_p, value_p)
-        fill(send, gain_f, key_f, value_f)
-
-    @pl.when(model_ref[0] != 0)
-    def _():
-        fill(keep, gain_f, key_f, value_f)
-        fill(send, gain_p, key_p, value_p)
-
-
-def partial_kernel(place_ref, packed, own_keep, own_got, pair_keep, pair_got, *outs_and_scratch):
+            out[plane, owner, :, features + per_head :] = side
+
+
+def partial_kernel(packed, own_keep, own_got, pair_keep, pair_got, *outs_and_scratch):
     outs, keys, values = outs_and_scratch[:-2], outs_and_scratch[-2], outs_and_scratch[-1]
-    plane, model, core = place_ref[0], place_ref[1], place_ref[2]
+    place, core = lax.axis_index("sp"), lax.axis_index("fsdp")
+    plane, model = place // 2, place % 2
     planes = len(outs)
     senders, tokens, _ = packed.shape
     length = senders * tokens
     rows = own_keep.shape[0] - GAIN_ROWS
     width = own_keep.shape[1] // 2
-    features = 4 * rows
     side = packed[:, :, packed.shape[2] - LANES :].reshape(length, LANES).astype(jnp.float32)
     inverse = side[:, 0:1] + side[:, 1:2] + side[:, 2:3]
     key_sum = value_sum = None
@@ -237,6 +255,14 @@
         )
 
 
+def here(x):
+    return pltpu.with_memory_space_constraint(x, pltpu.VMEM)
+
+
+def there(x):
+    return pltpu.with_memory_space_constraint(x, pltpu.HBM)
+
+
 def rotary_tables(length):
     half_dim = HEAD_DIM // 2
     frequency = jnp.exp(
@@ -259,63 +285,71 @@
     wide = depth // planes + per_head + LANES
     senders = 2 * planes
     length = senders * tokens
-    place = lax.axis_index("sp")
-    core = lax.axis_index("fsdp")
-    plane, model = place // 2, place % 2
     vmem = pl.BlockSpec(memory_space=pltpu.VMEM)
-    smem = pl.BlockSpec(memory_space=pltpu.SMEM)
 
     across = [(i, i ^ 1) for i in range(senders)]
     swap = [(0, 1), (1, 0)]
-    keep, send = pl.pallas_call(
-        weights_kernel,
-        out_shape=[jax.ShapeDtypeStruct((rows + GAIN_ROWS, 2 * width), jnp.bfloat16)] * 2,
-        in_specs=[smem] + [vmem] * 6,
-        out_specs=[vmem] * 2,
-        name="weights",
+    weights_shape = pltpu.VMEM((rows + GAIN_ROWS, 2 * width), jnp.bfloat16)
+    send, keep, packed = pl.pallas_call(
+        pack_kernel,
+        out_shape=[
+            weights_shape,
+            weights_shape,
+            pltpu.VMEM((planes, 2, tokens, wide), jnp.bfloat16),
+        ],
+        in_specs=[vmem] * 12,
+        out_specs=[vmem] * 3,
+        compiler_params=pltpu.CompilerParams(vmem_limit_bytes=KERNEL_BYTES),
+        name="pack",
     )(
-        model.reshape(1),
-        gain_p.reshape(1, rows),
-        key_p,
-        value_p,
-        gain_f.reshape(1, rows),
-        key_f,
-        value_f,
+        *(
+            there(array)
+            for array in (
+                gain_p,
+                key_p,
+                value_p,
+                gain_f,
+                key_f,
+                value_f,
+                hidden_p[0],
+                hidden_f[0],
+                queries_p[0],
+                queries_f[0],
+                docs_p,
+                docs_f,
+            )
+        ),
     )
     got = lax.ppermute(send, "sp", across)
-    packed = pl.pallas_call(
-        pack_kernel,
-        out_shape=jax.ShapeDtypeStruct((planes, 2, tokens, wide), jnp.bfloat16),
-        in_specs=[vmem] * 6,
-        out_specs=vmem,
-        name="pack",
-    )(hidden_p[0], hidden_f[0], queries_p[0], queries_f[0], docs_p, docs_f)
     packed = lax.all_to_all(
         packed.reshape(senders, tokens, wide), "sp", split_axis=0, concat_axis=0, tiled=True
     )
     pair_keep = lax.ppermute(keep, "fsdp", swap)
     pair_got = lax.ppermute(got, "fsdp", swap)
-    part_shape = jax.ShapeDtypeStruct((length, 2 * HEAD_DIM), jnp.float32)
+    part_shape = pltpu.VMEM((length, 2 * HEAD_DIM), jnp.float32)
+    packed = here(packed)
     parts = pl.pallas_call(
         partial_kernel,
         out_shape=[part_shape] * planes,
-        in_specs=[smem] + [vmem] * 5,
+        in_specs=[vmem] * 5,
         out_specs=[vmem] * planes,
         scratch_shapes=[pltpu.VMEM((planes, length, HEAD_DIM), jnp.float32)] * 2,
+        compiler_params=pltpu.CompilerParams(vmem_limit_bytes=KERNEL_BYTES),
         name="partial",
-    )(jnp.stack([plane, model, core]), packed, keep, got, pair_keep, pair_got)
+    )(packed, here(keep), here(got), here(pair_keep), here(pair_got))
     arrived = [parts[0]] + [
         lax.ppermute(parts[flip], "sp", [(i, i ^ (2 * flip)) for i in range(senders)])
-        for flip in range(1, planes)
+        for flip in reversed(range(1, planes))
     ]
     cosines, sines = rotary_tables(length)
     mixed = pl.pallas_call(
         attend_kernel,
-        out_shape=jax.ShapeDtypeStruct((senders, tokens, per_head), jnp.bfloat16),
+        out_shape=pltpu.VMEM((senders, tokens, per_head), jnp.bfloat16),
         in_specs=[vmem] * (3 + planes),
         out_specs=vmem,
+        compiler_params=pltpu.CompilerParams(vmem_limit_bytes=KERNEL_BYTES),
         name="attend",
-    )(packed, cosines, sines, *arrived)
+    )(packed, cosines, sines, *(here(part) for part in arrived))
     mixed = lax.all_to_all(mixed, "sp", split_axis=0, concat_axis=0, tiled=True)
     mixed = mixed.reshape(planes, 2, tokens, per_head).transpose(1, 2, 0, 3)
     mixed = mixed.reshape(2, 1, tokens, planes * per_head)
@@ -325,7 +359,7 @@
 def per_device(sp_size, fsdp_size, *arrays):
     policy, frozen = arrays[:6], arrays[6:]
     key_heads = policy[4].shape[1] // HEAD_DIM
-    tokens, depth = policy[0].shape[1:]
+    tokens, _ = policy[0].shape[1:]
     planes = sp_size // 2
     if (
         sp_size == 2 * key_heads

time: 83.3 us -> 74.9 us (0.90)
  waiting for transfers between devices: 35.2 us -> 43 us
  Pallas kernels: 11.3 us -> 4.48 us
  local copies, waits for them, and re-layouts: 5.64 us -> 1.28 us
  blocking collectives: 14.3 us -> 10.8 us
  other arithmetic: 2.06 us -> 0.68 us
    pallas_call x3 -> x2, Pallas kernels: 7.68 us -> 3.57 us  [the longest x1 2.57 us: planes_contract(): pl.pallas_call(pack_kernel, out_shape=[weights_shape, weights_shape, pltp...]
    ppermute x1, waiting for transfers between devices: 16.3 us -> 20 us  [planes_contract(): got = lax.ppermute(send, 'sp', across)]
    all_to_all x1, blocking collectives: 14.3 us -> 10.8 us  [planes_contract(): mixed = lax.all_to_all(mixed, 'sp', split_axis=0, concat_axis=0, tiled=True)]
    ppermute x3, waiting for transfers between devices: 17.7 us -> 21 us  [planes_contract(): lax.ppermute(parts[flip], 'sp', [(i, i ^ 2 * flip) for i in range(senders)])]
    unnamed x19 -> x1, local copies, waits for them, and re-layouts: 3.24 us -> 0.01 us
    pallas_call x1, Pallas kernels: 3.65 us -> 0.91 us  [planes_contract(): pl.pallas_call(partial_kernel, out_shape=[part_shape] * planes, in_specs=...]
    reshape x2 -> x0, local copies, waits for them, and re-layouts: 1.13 us -> none  [the longest x1 0.56 us: planes_contract(): gain_p.reshape(1, rows)]
  transfers between devices with their start and end apart: 7 -> 7, of which waited for: 4 -> 4; matrix products, arithmetic and copies ran while one was open for 4% -> 1% of each run, Pallas kernels for 3% -> 0%
where the time goes in v2:
time: 74.9 us; the launch traced here: 74.6 us
  waiting for transfers between devices  43 us (57%)
  starting transfers between devices  13.8 us (18%)
  blocking collectives  10.8 us (14%)
  Pallas kernels  4.48 us (6%)
  local copies, waits for them, and re-layouts  1.28 us (2%)
    ppermute x3, waiting for transfers between devices, planes_contract(): lax.ppermute(parts[flip], 'sp', [(i, i ^ 2 * flip) for i in range(senders)])  21 us
    ppermute x1, waiting for transfers between devices, planes_contract(): got = lax.ppermute(send, 'sp', across)  20 us
    all_to_all x1, blocking collectives, planes_contract(): mixed = lax.all_to_all(mixed, 'sp', split_axis=0, concat_axis=0, tiled=True)  10.8 us
    all_to_all x1, starting transfers between devices, planes_contract(): lax.all_to_all(packed.reshape(senders, tokens, wide), 'sp', split_axis=0,...  7.31 us
    ppermute x3, starting transfers between devices, planes_contract(): lax.ppermute(parts[flip], 'sp', [(i, i ^ 2 * flip) for i in range(senders)])  4.45 us
    pallas_call x1, Pallas kernels, planes_contract(): pl.pallas_call(pack_kernel, out_shape=[weights_shape, weights_shape, pltp...  2.57 us
    ppermute x1, starting transfers between devices, planes_contract(): got = lax.ppermute(send, 'sp', across)  2.02 us
    ppermute x1, waiting for transfers between devices, planes_contract(): pair_got = lax.ppermute(got, 'fsdp', swap)  1.92 us
  transfers between devices with their start and end apart: 7, of which 4 were waited for; matrix products, arithmetic and copies ran while one was open for 1% of the time, Pallas kernels for 0%

profile of v2, /device:TPU:0, one launch (start us, length us, event | category | flops | bytes accessed | tf_op | source)
XLA Modules:
  0.0 74.6 jit_solution(5960656909695814496)
XLA Ops:
  0.6 2.6 %pack.1 = (bf16[272,1024]{1,0:T(8,128)(2,1)S(1)}, bf16[272,1024]{1,0:T(8,128)(2,1)S(1)}, bf16[4,2,32,1408]{3,2,1,0:T(8,128)(2,1)}) custom-call(bf16[256]{0:T(256)(128)(2,1)} %gain_p.1, bf16[256,512]{1,0:T(8,128)(2,1)} %key_p.1, bf16[256,512]{1,0:T(8,128)(2,1)} %value_p.1, bf16[256]{0:T(256)(128)(2,1)} %gain_f.1, bf16[256,512]{1,0:T(8,128)(2,1)} %key_f.1, ...), custom_call_target="tpu_custom_call" | custom-call | tf_op jit(solution)/shard_map/pack/pallas_call | solution.py:293
  3.2 7.3 %all-to-all-start = ((bf16[8,32,1408]{2,1,0:T(8,128)(2,1)}), bf16[8,32,1408]{2,1,0:T(8,128)(2,1)S(1)}, u32[]{:S(2)}, u32[]{:S(2)}) async-start(bf16[8,32,1408]{2,1,0:T(8,128)(2,1)} %bitcast.4), calls=%async_computation | async-start | bytes 1441792 | tf_op jit(solution)/shard_map/all_to_all | solution.py:324
  10.5 2.0 %collective-permute-start = (bf16[272,1024]{1,0:T(8,128)(2,1)S(1)}, bf16[272,1024]{1,0:T(8,128)(2,1)S(1)}, u32[]{:S(2)}, u32[]{:S(2)}) collective-permute-start(bf16[272,1024]{1,0:T(8,128)(2,1)S(1)} %get-tuple-element.11), channel_id=1, source_target_pairs={{0,2},{2,0},{4,6},{6,4},{8,10},{10,8},{12,14},{14,12},{1,3},{3,1},... | collective-permute-start | bytes 1671176 | tf_op jit(solution)/shard_map/ppermute | solution.py:323
  12.5 0.0 collective-permute-start.1
  12.5 20.0 %collective-permute-done.own_got = bf16[272,1024]{1,0:T(8,128)(2,1)S(1)} collective-permute-done((bf16[272,1024]{1,0:T(8,128)(2,1)S(1)}, bf16[272,1024]{1,0:T(8,128)(2,1)S(1)}, u32[]{:S(2)}, u32[]{:S(2)}) %collective-permute-start) | collective-permute-done | bytes 557088 | tf_op jit(solution)/shard_map/ppermute | solution.py:323
  32.5 0.0 collective-permute-start.2
  32.5 0.0 collective-permute-done.1.pair_keep
  32.6 1.9 %collective-permute-done.2.pair_got = bf16[272,1024]{1,0:T(8,128)(2,1)S(1)} collective-permute-done((bf16[272,1024]{1,0:T(8,128)(2,1)S(1)}, bf16[272,1024]{1,0:T(8,128)(2,1)S(1)}, u32[]{:S(2)}, u32[]{:S(2)}) %collective-permute-start.2) | collective-permute-done | bytes 557088 | tf_op jit(solution)/shard_map/ppermute | solution.py:328
  34.5 0.0 all-to-all-done.packed
  34.5 0.9 %partial.1 = (f32[256,256]{1,0:T(8,128)S(1)}, f32[256,256]{1,0:T(8,128)S(1)}, f32[256,256]{1,0:T(8,128)S(1)}, f32[256,256]{1,0:T(8,128)S(1)}) custom-call(bf16[8,32,1408]{2,1,0:T(8,128)(2,1)S(1)} %all-to-all-done.packed, bf16[272,1024]{1,0:T(8,128)(2,1)S(1)} %get-tuple-element.10.own_keep, bf16[272,1024]{1,0:T(8,128)(2,1)S(1)} %collective-permute-done.own_got, ...), custom_call_target="tpu_custom_call" | custom-call | tf_op jit(solution)/shard_map/partial/pallas_call | solution.py:331
  35.4 3.3 %collective-permute-start.3 = (f32[256,256]{1,0:T(8,128)S(1)}, f32[256,256]{1,0:T(8,128)S(1)}, u32[]{:S(2)}, u32[]{:S(2)}) collective-permute-start(f32[256,256]{1,0:T(8,128)S(1)} %get-tuple-element.13), channel_id=1, source_target_pairs={{0,12},{2,14},{4,8},{6,10},{8,4},{10,6},{12,0},{14,2},{1,13},{3,15... | collective-permute-start | bytes 786440 | tf_op jit(solution)/shard_map/ppermute | solution.py:341
  38.7 0.0 collective-permute-start.4
  38.7 1.1 %collective-permute-start.5 = (f32[256,256]{1,0:T(8,128)S(1)}, f32[256,256]{1,0:T(8,128)S(1)}, u32[]{:S(2)}, u32[]{:S(2)}) collective-permute-start(f32[256,256]{1,0:T(8,128)S(1)} %get-tuple-element.15), channel_id=1, source_target_pairs={{0,4},{2,6},{4,0},{6,2},{8,12},{10,14},{12,8},{14,10},{1,5},{3,7},... | collective-permute-start | bytes 786440 | tf_op jit(solution)/shard_map/ppermute | solution.py:341
  39.9 0.5 fusion
  40.4 0.1 pad_maximum_fusion
  40.5 6.1 %collective-permute-done.3.parts_and_out_1_ = f32[256,256]{1,0:T(8,128)S(1)} collective-permute-done((f32[256,256]{1,0:T(8,128)S(1)}, f32[256,256]{1,0:T(8,128)S(1)}, u32[]{:S(2)}, u32[]{:S(2)}) %collective-permute-start.3) | collective-permute-done | bytes 262176 | tf_op jit(solution)/shard_map/ppermute | solution.py:341
  46.6 15.0 %collective-permute-done.4.parts_and_out_2_ = f32[256,256]{1,0:T(8,128)S(1)} collective-permute-done((f32[256,256]{1,0:T(8,128)S(1)}, f32[256,256]{1,0:T(8,128)S(1)}, u32[]{:S(2)}, u32[]{:S(2)}) %collective-permute-start.4) | collective-permute-done | bytes 262176 | tf_op jit(solution)/shard_map/ppermute | solution.py:341
  61.6 0.0 collective-permute-done.5.parts_and_out_3_
  61.6 1.0 %attend.1 = bf16[8,32,256]{2,1,0:T(8,128)(2,1)S(1)} custom-call(bf16[8,32,1408]{2,1,0:T(8,128)(2,1)S(1)} %all-to-all-done.packed, f32[256,128]{1,0:T(8,128)S(1)} %get-tuple-element.21.cosines, f32[256,128]{1,0:T(8,128)S(1)} %get-tuple-element.22.sines, f32[256,256]{1,0:T(8,128)S(1)} %get-tuple-element.12.parts_and_out_0_, ...), custom_call_target="tpu_custom_call" | custom-call | tf_op jit(solution)/shard_map/attend/pallas_call | solution.py:345
  62.6 10.8 %all_to_all.10 = bf16[8,32,256]{2,1,0:T(8,128)(2,1)S(1)} all-to-all(bf16[8,32,256]{2,1,0:T(8,128)(2,1)S(1)} %attend.1), channel_id=1, replica_groups=mesh['groups'=2,'sp'=8,'fsdp'=2] {'sp'}, dimensions={0} | all-to-all | bytes 262144 | tf_op jit(solution)/shard_map/all_to_all | solution.py:353
  73.4 0.6 copy.17
  74.0 0.6 copy.16
  (3 shorter events, 0.0 us)
Async XLA Ops:
  3.2 31.3 %all-to-all-start = ((bf16[8,32,1408]{2,1,0:T(8,128)(2,1)}), bf16[8,32,1408]{2,1,0:T(8,128)(2,1)S(1)}, u32[]{:S(2)}, u32[]{:S(2)}) async-start(bf16[8,32,1408]{2,1,0:T(8,128)(2,1)} %bitcast.4), calls=%async_computation | async-start | bytes 1441792 | tf_op jit(solution)/shard_map/all_to_all | solution.py:324
  10.5 22.0 %collective-permute-start = (bf16[272,1024]{1,0:T(8,128)(2,1)S(1)}, bf16[272,1024]{1,0:T(8,128)(2,1)S(1)}, u32[]{:S(2)}, u32[]{:S(2)}) collective-permute-start(bf16[272,1024]{1,0:T(8,128)(2,1)S(1)} %get-tuple-element.11), channel_id=1, source_target_pairs={{0,2},{2,0},{4,6},{6,4},{8,10},{10,8},{12,14},{14,12},{1,3},{3,1},... | collective-permute-start | bytes 1671176 | tf_op jit(solution)/shard_map/ppermute | solution.py:323
  12.5 20.0 %collective-permute-start.1 = (bf16[272,1024]{1,0:T(8,128)(2,1)S(1)}, bf16[272,1024]{1,0:T(8,128)(2,1)S(1)}, u32[]{:S(2)}, u32[]{:S(2)}) collective-permute-start(bf16[272,1024]{1,0:T(8,128)(2,1)S(1)} %get-tuple-element.10.own_keep), channel_id=1, source_target_pairs={{0,1},{1,0},{2,3},{3,2},{4,5},{5,4},{6,7},{7,6},{8,9},{9,8},{10,11... | collective-permute-start | bytes 1671176 | tf_op jit(solution)/shard_map/ppermute | solution.py:327
  32.5 2.0 %collective-permute-start.2 = (bf16[272,1024]{1,0:T(8,128)(2,1)S(1)}, bf16[272,1024]{1,0:T(8,128)(2,1)S(1)}, u32[]{:S(2)}, u32[]{:S(2)}) collective-permute-start(bf16[272,1024]{1,0:T(8,128)(2,1)S(1)} %collective-permute-done.own_got), channel_id=1, source_target_pairs={{0,1},{1,0},{2,3},{3,2},{4,5},{5,4},{6,7},{7,6},{8,9},{9,8},{10,11... | collective-permute-start | bytes 1671176 | tf_op jit(solution)/shard_map/ppermute | solution.py:328
  35.4 11.2 %collective-permute-start.3 = (f32[256,256]{1,0:T(8,128)S(1)}, f32[256,256]{1,0:T(8,128)S(1)}, u32[]{:S(2)}, u32[]{:S(2)}) collective-permute-start(f32[256,256]{1,0:T(8,128)S(1)} %get-tuple-element.13), channel_id=1, source_target_pairs={{0,12},{2,14},{4,8},{6,10},{8,4},{10,6},{12,0},{14,2},{1,13},{3,15... | collective-permute-start | bytes 786440 | tf_op jit(solution)/shard_map/ppermute | solution.py:341
  38.7 22.8 %collective-permute-start.4 = (f32[256,256]{1,0:T(8,128)S(1)}, f32[256,256]{1,0:T(8,128)S(1)}, u32[]{:S(2)}, u32[]{:S(2)}) collective-permute-start(f32[256,256]{1,0:T(8,128)S(1)} %get-tuple-element.14), channel_id=1, source_target_pairs={{0,8},{2,10},{4,12},{6,14},{8,0},{10,2},{12,4},{14,6},{1,9},{3,11}... | collective-permute-start | bytes 786440 | tf_op jit(solution)/shard_map/ppermute | solution.py:341
  38.7 22.8 %collective-permute-start.5 = (f32[256,256]{1,0:T(8,128)S(1)}, f32[256,256]{1,0:T(8,128)S(1)}, u32[]{:S(2)}, u32[]{:S(2)}) collective-permute-start(f32[256,256]{1,0:T(8,128)S(1)} %get-tuple-element.15), channel_id=1, source_target_pairs={{0,4},{2,6},{4,0},{6,2},{8,12},{10,14},{12,8},{14,10},{1,5},{3,7},... | collective-permute-start | bytes 786440 | tf_op jit(solution)/shard_map/ppermute | solution.py:341

commit v3 on v2

--- a/solution.py
+++ b/solution.py
@@ -15,7 +15,8 @@
 ROPE_BASE = 500000.0
 MASKED = -1e30
 LANES = 128
-GAIN_ROWS = 16
+SIDE_ROWS = 8
+SIDE_GAINS = 4
 KERNEL_BYTES = 16 * 2**20
 
 
@@ -118,110 +119,180 @@
     return (run_model(*policy), run_model(*frozen))
 
 
+def weights_kernel(key_p, value_p, key_f, value_f, send, keep, sems):
+    _, width = key_p.shape
+    half = send.shape[0]
+    model = lax.axis_index("sp") // (lax.axis_size("sp") // 2)
+    first = pl.multiple_of(lax.axis_index("groups") * half, half)
+
+    def move(key_own, value_own, key_other, value_other):
+        copies = [
+            pltpu.make_async_copy(source, target, sems.at[index])
+            for index, (source, target) in enumerate(
+                (
+                    (key_other.at[pl.ds(first, half), :], send.at[:, :width]),
+                    (value_other.at[pl.ds(first, half), :], send.at[:, width:]),
+                    (key_own, keep.at[:, :width]),
+                    (value_own, keep.at[:, width:]),
+                )
+            )
+        ]
+        for copy in copies:
+            copy.start()
+        for copy in copies:
+            copy.wait()
+
+    @pl.when(model == 0)
+    def _():
+        move(key_p, value_p, key_f, value_f)
+
+    @pl.when(model != 0)
+    def _():
+        move(key_f, value_f, key_p, value_p)
+
+
 def pack_kernel(
     gain_p,
-    key_p,
-    value_p,
     gain_f,
-    key_f,
-    value_f,
+    pair_gain_p,
+    pair_gain_f,
     hidden_p,
     hidden_f,
     queries_p,
     queries_f,
     docs_p,
     docs_f,
-    send,
-    keep,
     out,
 ):
-    rows, width = key_p.shape
-
-    def fill(target, gain, key, value):
-        target[:rows, :width] = key[...]
-        target[:rows, width:] = value[...]
-        target[rows:, :rows] = jnp.broadcast_to(gain[...].reshape(1, rows), (GAIN_ROWS, rows))
-
-    model = lax.axis_index("sp") % 2
-
-    @pl.when(model == 0)
-    def _():
-        fill(send, gain_f, key_f, value_f)
-        fill(keep, gain_p, key_p, value_p)
-
-    @pl.when(model != 0)
-    def _():
-        fill(send, gain_p, key_p, value_p)
-        fill(keep, gain_f, key_f, value_f)
-
-    planes, _, tokens, _ = out.shape
-    features = hidden_p.shape[1] // planes
-    per_head = queries_p.shape[1] // planes
-    lane = lax.broadcasted_iota(jnp.int32, (tokens, LANES), 1)
-    diagonal = lax.broadcasted_iota(jnp.int32, (tokens, tokens), 0) == lax.broadcasted_iota(
-        jnp.int32, (tokens, tokens), 1
-    )
-    for owner, (hidden, queries, docs) in enumerate(
-        ((hidden_p, queries_p, docs_p), (hidden_f, queries_f, docs_f))
+    _, units, _, _ = out.shape
+    tokens, depth = hidden_p.shape
+    rows = gain_p.shape[0]
+    block = 2 * rows
+    tiles = block // LANES
+    per_head = queries_p.shape[1] // units
+    row = lax.broadcasted_iota(jnp.int32, (SIDE_ROWS, LANES), 0)
+    diagonal = lax.broadcasted_iota(jnp.int32, (tokens, LANES), 0) == lax.broadcasted_iota(
+        jnp.int32, (tokens, LANES), 1
+    )
+
+    def turned(column):
+        return jnp.sum(jnp.where(diagonal, column, 0.0), axis=0, keepdims=True)
+
+    for owner, (hidden, queries, docs, gain, pair_gain) in enumerate(
+        (
+            (hidden_p, queries_p, docs_p, gain_p, pair_gain_p),
+            (hidden_f, queries_f, docs_f, gain_f, pair_gain_f),
+        )
     ):
         widened = hidden[...].astype(jnp.float32)
-        mean = jnp.sum(widened * widened, axis=-1, keepdims=True) * (1.0 / hidden.shape[1])
+        mean = jnp.sum(widened * widened, axis=-1, keepdims=True) * (1.0 / depth)
         inverse = lax.rsqrt(mean + EPS)
         high = inverse.astype(jnp.bfloat16).astype(jnp.float32)
         middle = (inverse - high).astype(jnp.bfloat16).astype(jnp.float32)
         low = inverse - high - middle
-        doc = jnp.sum(
-            jnp.where(diagonal, docs[...].astype(jnp.float32), 0.0), axis=-1, keepdims=True
-        )
-        side = jnp.where(lane == 0, high, 0.0)
-        side = jnp.where(lane == 1, middle, side)
-        side = jnp.where(lane == 2, low, side)
-        side = jnp.where(lane == 3, doc, side).astype(jnp.bfloat16)
-        for plane in range(planes):
-            out[plane, owner, :, :features] = hidden[:, plane * features : (plane + 1) * features]
-            out[plane, owner, :, features : features + per_head] = queries[
-                :, plane * per_head : (plane + 1) * per_head
-            ]
-            out[plane, owner, :, features + per_head :] = side
-
-
-def partial_kernel(packed, own_keep, own_got, pair_keep, pair_got, *outs_and_scratch):
+        doc = jnp.concatenate(
+            [docs[...].astype(jnp.float32), jnp.zeros((1, LANES - tokens), jnp.float32)], axis=-1
+        )
+        gains = [gain[...].reshape(1, rows).astype(jnp.float32)]
+        gains.append(pair_gain[...].reshape(1, rows).astype(jnp.float32))
+        side = jnp.where(row == 0, turned(high), 0.0)
+        side = jnp.where(row == 1, turned(middle), side)
+        side = jnp.where(row == 2, turned(low), side)
+        side = jnp.where(row == 3, doc, side)
+        for which in range(2):
+            for part in range(rows // LANES):
+                side = jnp.where(
+                    row == SIDE_GAINS + which * (rows // LANES) + part,
+                    gains[which][:, part * LANES : (part + 1) * LANES],
+                    side,
+                )
+        side = side.astype(jnp.bfloat16)
+        for unit in range(units):
+            for tile in range(2 * tiles):
+                first = (unit + (tile // tiles) * units) * block + (tile % tiles) * LANES
+                out[owner, unit, tile * tokens : (tile + 1) * tokens, :] = hidden[
+                    :, first : first + LANES
+                ]
+            for tile in range(per_head // LANES):
+                first = unit * per_head + tile * LANES
+                low = (2 * tiles + tile) * tokens
+                out[owner, unit, low : low + tokens, :] = queries[:, first : first + LANES]
+            out[owner, unit, out.shape[2] - SIDE_ROWS :, :] = side
+
+
+def side_columns(packed, tokens, sums):
+    senders, high, _ = packed.shape
+    side = packed[:, high - SIDE_ROWS :, :].reshape(senders * SIDE_ROWS, LANES)
+    turned = jnp.transpose(side.astype(jnp.float32))
+    columns = []
+    for sender in range(senders):
+        column = None
+        for index in sums:
+            first = sender * SIDE_ROWS + index
+            part = turned[:tokens, first : first + 1]
+            column = part if column is None else column + part
+        columns.append(column)
+    return jnp.concatenate(columns, axis=0)
+
+
+def partial_kernel(
+    tokens, packed, keep, got, far, pair_keep, pair_got, pair_far, *outs_and_scratch
+):
     outs, keys, values = outs_and_scratch[:-2], outs_and_scratch[-2], outs_and_scratch[-1]
-    place, core = lax.axis_index("sp"), lax.axis_index("fsdp")
-    plane, model = place // 2, place % 2
-    planes = len(outs)
-    senders, tokens, _ = packed.shape
+    units = len(outs)
+    place, core, group = lax.axis_index("sp"), lax.axis_index("fsdp"), lax.axis_index("groups")
+    model, unit = place // units, place % units
+    senders, high, _ = packed.shape
     length = senders * tokens
-    rows = own_keep.shape[0] - GAIN_ROWS
-    width = own_keep.shape[1] // 2
-    side = packed[:, :, packed.shape[2] - LANES :].reshape(length, LANES).astype(jnp.float32)
-    inverse = side[:, 0:1] + side[:, 1:2] + side[:, 2:3]
+    half = got.shape[0]
+    width = keep.shape[1] // 2
+    halves = keep.shape[0] // half
+    strips = half // LANES
+    inverse = side_columns(packed, tokens, (0, 1, 2))
+    first_side = high - SIDE_ROWS
     key_sum = value_sum = None
-    for flip_core, flip_model, block in (
-        (0, 0, own_keep),
-        (0, 1, own_got),
-        (1, 0, pair_keep),
-        (1, 1, pair_got),
+    for weights, flip_model, flip_core, part in (
+        (keep, 0, 0, 0),
+        (keep, 0, 0, 1),
+        (got, 1, 0, group),
+        (far, 1, 0, 1 - group),
+        (pair_keep, 0, 1, 0),
+        (pair_keep, 0, 1, 1),
+        (pair_got, 1, 1, group),
+        (pair_far, 1, 1, 1 - group),
     ):
-        first = pl.multiple_of(((model ^ flip_model) * 2 + (core ^ flip_core)) * rows, rows)
-        hidden = packed[:, :, pl.ds(first, rows)].reshape(length, rows).astype(jnp.float32)
-        gain = block[rows : rows + 1, :rows].astype(jnp.float32)
-        normed = (hidden * inverse * gain).astype(jnp.bfloat16)
-        key_part = jnp.dot(normed, block[:rows, :width], preferred_element_type=jnp.float32)
-        value_part = jnp.dot(normed, block[:rows, width:], preferred_element_type=jnp.float32)
+        source = model ^ flip_model
+        side = packed[source * units + unit, first_side:, :].astype(jnp.float32)
+        columns = []
+        for strip in range(strips):
+            tile = ((source * 2 + (core ^ flip_core)) * halves + part) * strips + strip
+            hidden = packed[:, pl.ds(pl.multiple_of(tile * tokens, tokens), tokens), :]
+            hidden = hidden.reshape(length, LANES).astype(jnp.float32)
+            wanted = SIDE_GAINS + (flip_core * halves + part) * strips + strip
+            picked = lax.broadcasted_iota(jnp.int32, (SIDE_ROWS, LANES), 0) == wanted
+            gain = jnp.sum(jnp.where(picked, side, 0.0), axis=0, keepdims=True)
+            columns.append((hidden * inverse * gain).astype(jnp.bfloat16))
+        normed = jnp.concatenate(columns, axis=-1) if strips > 1 else columns[0]
+        low = part * half if weights is keep or weights is pair_keep else 0
+        key_part = jnp.dot(
+            normed, weights[low : low + half, :width], preferred_element_type=jnp.float32
+        )
+        value_part = jnp.dot(
+            normed, weights[low : low + half, width:], preferred_element_type=jnp.float32
+        )
         key_sum = key_part if key_sum is None else key_sum + key_part
         value_sum = value_part if value_sum is None else value_sum + value_part
-    for head in range(planes):
+    for head in range(units):
         keys[head] = key_sum[:, head * HEAD_DIM : (head + 1) * HEAD_DIM]
         values[head] = value_sum[:, head * HEAD_DIM : (head + 1) * HEAD_DIM]
-    for flip in range(planes):
-        outs[flip][:, :HEAD_DIM] = keys[plane ^ flip]
-        outs[flip][:, HEAD_DIM:] = values[plane ^ flip]
-
-
-def attend_kernel(packed, cosines, sines, *parts_and_out):
+    for flip in range(units):
+        outs[flip][:, :HEAD_DIM] = keys[unit ^ flip]
+        outs[flip][:, HEAD_DIM:] = values[unit ^ flip]
+
+
+def attend_kernel(tokens, packed, cosines, sines, *parts_and_out):
     parts, out = parts_and_out[:-1], parts_and_out[-1]
-    senders, tokens, wide = packed.shape
+    senders = packed.shape[0]
     length = senders * tokens
     per_head = out.shape[2]
     total = parts[0][...]
@@ -233,15 +304,14 @@
     )
     keys = (raw_keys * cosines[...] + turned * sines[...]).astype(jnp.bfloat16)
     values = total[:, HEAD_DIM:].astype(jnp.bfloat16)
-    side = packed[:, :, wide - LANES :].reshape(length, LANES).astype(jnp.float32)
-    query_docs = side[:, 3:4]
-    key_docs = jnp.transpose(side)[3:4, :]
+    query_docs = side_columns(packed, tokens, (3,))
+    key_docs = jnp.transpose(jnp.broadcast_to(query_docs, (length, LANES)))[:1, :]
     row = lax.broadcasted_iota(jnp.int32, (length, length), 0)
     column = lax.broadcasted_iota(jnp.int32, (length, length), 1)
     allowed = (column <= row) & (query_docs == key_docs)
     for head in range(per_head // HEAD_DIM):
-        first = wide - LANES - per_head + head * HEAD_DIM
-        queries = packed[:, :, first : first + HEAD_DIM].reshape(length, HEAD_DIM)
+        low = packed.shape[1] - SIDE_ROWS - (per_head // HEAD_DIM - head) * tokens
+        queries = packed[:, low : low + tokens, :].reshape(length, HEAD_DIM)
         scores = lax.dot_general(
             queries, keys, (((1,), (1,)), ((), ())), preferred_element_type=jnp.float32
         ) * (HEAD_DIM ** (-0.5))
@@ -259,6 +329,13 @@
     return pltpu.with_memory_space_constraint(x, pltpu.VMEM)
 
 
+def assemble_kernel(arrived, out_p, out_f):
+    _, units, _, per_head = arrived.shape
+    for owner, out in enumerate((out_p, out_f)):
+        for unit in range(units):
+            out[:, unit * per_head : (unit + 1) * per_head] = arrived[owner, unit]
+
+
 def there(x):
     return pltpu.with_memory_space_constraint(x, pltpu.HBM)
 
@@ -276,41 +353,51 @@
     )
 
 
-def planes_contract(planes, policy, frozen):
+def halves_contract(units, policy, frozen):
     hidden_p, queries_p, docs_p, gain_p, key_p, value_p = policy
     hidden_f, queries_f, docs_f, gain_f, key_f, value_f = frozen
-    tokens, depth = hidden_p.shape[1:]
+    tokens = hidden_p.shape[1]
     rows, width = key_p.shape
-    per_head = queries_p.shape[2] // planes
-    wide = depth // planes + per_head + LANES
-    senders = 2 * planes
+    half = rows // 2
+    per_head = queries_p.shape[2] // units
+    senders = 2 * units
     length = senders * tokens
+    high = (4 * rows + per_head) // LANES * tokens + SIDE_ROWS
     vmem = pl.BlockSpec(memory_space=pltpu.VMEM)
-
-    across = [(i, i ^ 1) for i in range(senders)]
+    hbm = pl.BlockSpec(memory_space=pltpu.HBM)
+    params = pltpu.CompilerParams(vmem_limit_bytes=KERNEL_BYTES)
     swap = [(0, 1), (1, 0)]
-    weights_shape = pltpu.VMEM((rows + GAIN_ROWS, 2 * width), jnp.bfloat16)
-    send, keep, packed = pl.pallas_call(
+
+    send, keep = pl.pallas_call(
+        weights_kernel,
+        out_shape=[
+            pltpu.VMEM((half, 2 * width), jnp.bfloat16),
+            pltpu.VMEM((rows, 2 * width), jnp.bfloat16),
+        ],
+        in_specs=[hbm] * 4,
+        out_specs=[vmem] * 2,
+        scratch_shapes=[pltpu.SemaphoreType.DMA((4,))],
+        compiler_params=params,
+        name="weights",
+    )(*(there(array) for array in (key_p, value_p, key_f, value_f)))
+    got = lax.ppermute(send, "sp", [(i, i ^ units) for i in range(senders)])
+    pair_gain_p = lax.ppermute(gain_p, "fsdp", swap)
+    pair_gain_f = lax.ppermute(gain_f, "fsdp", swap)
+    packed = pl.pallas_call(
         pack_kernel,
-        out_shape=[
-            weights_shape,
-            weights_shape,
-            pltpu.VMEM((planes, 2, tokens, wide), jnp.bfloat16),
-        ],
-        in_specs=[vmem] * 12,
-        out_specs=[vmem] * 3,
-        compiler_params=pltpu.CompilerParams(vmem_limit_bytes=KERNEL_BYTES),
+        out_shape=pltpu.VMEM((2, units, high, LANES), jnp.bfloat16),
+        in_specs=[vmem] * 10,
+        out_specs=vmem,
+        compiler_params=params,
         name="pack",
     )(
         *(
             there(array)
             for array in (
                 gain_p,
-                key_p,
-                value_p,
                 gain_f,
-                key_f,
-                value_f,
+                pair_gain_p,
+                pair_gain_f,
                 hidden_p[0],
                 hidden_f[0],
                 queries_p[0],
@@ -318,65 +405,75 @@
                 docs_p,
                 docs_f,
             )
-        ),
-    )
-    got = lax.ppermute(send, "sp", across)
+        )
+    )
     packed = lax.all_to_all(
-        packed.reshape(senders, tokens, wide), "sp", split_axis=0, concat_axis=0, tiled=True
-    )
+        packed.reshape(senders, high, LANES), "sp", split_axis=0, concat_axis=0, tiled=True
+    )
+    far = lax.ppermute(got, "groups", swap)
     pair_keep = lax.ppermute(keep, "fsdp", swap)
     pair_got = lax.ppermute(got, "fsdp", swap)
-    part_shape = pltpu.VMEM((length, 2 * HEAD_DIM), jnp.float32)
+    pair_far = lax.ppermute(far, "fsdp", swap)
     packed = here(packed)
     parts = pl.pallas_call(
-        partial_kernel,
-        out_shape=[part_shape] * planes,
-        in_specs=[vmem] * 5,
-        out_specs=[vmem] * planes,
-        scratch_shapes=[pltpu.VMEM((planes, length, HEAD_DIM), jnp.float32)] * 2,
-        compiler_params=pltpu.CompilerParams(vmem_limit_bytes=KERNEL_BYTES),
+        functools.partial(partial_kernel, tokens),
+        out_shape=[pltpu.VMEM((length, 2 * HEAD_DIM), jnp.float32)] * units,
+        in_specs=[vmem] * 7,
+        out_specs=[vmem] * units,
+        scratch_shapes=[pltpu.VMEM((units, length, HEAD_DIM), jnp.float32)] * 2,
+        compiler_params=params,
         name="partial",
-    )(packed, here(keep), here(got), here(pair_keep), here(pair_got))
-    arrived = [parts[0]] + [
-        lax.ppermute(parts[flip], "sp", [(i, i ^ (2 * flip)) for i in range(senders)])
-        for flip in reversed(range(1, planes))
-    ]
+    )(packed, *(here(array) for array in (keep, got, far, pair_keep, pair_got, pair_far)))
+    arrived = [parts[0]]
+    for flip in range(1, units):
+        arrived.append(
+            lax.ppermute(parts[flip], "sp", [(i, i ^ flip) for i in range(senders)])
+        )
     cosines, sines = rotary_tables(length)
     mixed = pl.pallas_call(
-        attend_kernel,
+        functools.partial(attend_kernel, tokens),
         out_shape=pltpu.VMEM((senders, tokens, per_head), jnp.bfloat16),
-        in_specs=[vmem] * (3 + planes),
+        in_specs=[vmem] * (3 + units),
         out_specs=vmem,
-        compiler_params=pltpu.CompilerParams(vmem_limit_bytes=KERNEL_BYTES),
+        compiler_params=params,
         name="attend",
     )(packed, cosines, sines, *(here(part) for part in arrived))
     mixed = lax.all_to_all(mixed, "sp", split_axis=0, concat_axis=0, tiled=True)
-    mixed = mixed.reshape(planes, 2, tokens, per_head).transpose(1, 2, 0, 3)
-    mixed = mixed.reshape(2, 1, tokens, planes * per_head)
-    return (mixed[0], mixed[1])
-
-
-def per_device(sp_size, fsdp_size, *arrays):
+    out_shape = jax.ShapeDtypeStruct((tokens, units * per_head), jnp.bfloat16)
+    mixed_p, mixed_f = pl.pallas_call(
+        assemble_kernel,
+        out_shape=[out_shape] * 2,
+        in_specs=[vmem],
+        out_specs=[vmem] * 2,
+        compiler_params=params,
+        name="assemble",
+    )(here(mixed.reshape(2, units, tokens, per_head)))
+    return (mixed_p[None], mixed_f[None])
+
+
+def per_device(groups, sp_size, fsdp_size, *arrays):
     policy, frozen = arrays[:6], arrays[6:]
     key_heads = policy[4].shape[1] // HEAD_DIM
-    tokens, _ = policy[0].shape[1:]
-    planes = sp_size // 2
+    tokens = policy[0].shape[1]
+    rows = policy[4].shape[0]
     if (
         sp_size == 2 * key_heads
-        and planes & (planes - 1) == 0
+        and key_heads & (key_heads - 1) == 0
+        and groups == 2
         and fsdp_size == 2
         and tokens % 16 == 0
-        and policy[4].shape[0] % LANES == 0
-        and 2 * policy[4].shape[0] <= 2 * policy[4].shape[1]
+        and tokens <= LANES
+        and rows % (2 * LANES) == 0
+        and SIDE_GAINS + 2 * rows // LANES <= SIDE_ROWS
         and sp_size * tokens <= 512
     ):
-        return planes_contract(planes, policy, frozen)
+        return halves_contract(key_heads, policy, frozen)
     return gathered_weights(policy, frozen)
 
 
 def solution(mesh):
     return jax.shard_map(
-        functools.partial(per_device, mesh.shape["sp"], mesh.shape["fsdp"]),
+        functools.partial(per_device, *(mesh.shape[axis] for axis in ("groups", "sp", "fsdp"))),
         mesh=mesh,
         in_specs=(
             P(("groups", "fsdp"), "sp", None),

time: 74.9 us -> 81.1 us (1.083)
  Pallas kernels: 4.48 us -> 6.82 us
  starting transfers between devices: 13.8 us -> 15.7 us
  waiting for transfers between devices: 43 us -> 44.8 us
    pallas_call x3 -> x5, Pallas kernels: 4.48 us -> 6.82 us  [the longest x1 2.23 us: halves_contract(): pl.pallas_call(pack_kernel, out_shape=pltpu.VMEM((2, units, high, LANES),...]
    ppermute x6 -> x10, starting transfers between devices: 6.48 us -> 8.67 us  [the longest x3 3.55 us: halves_contract(): lax.ppermute(parts[flip], 'sp', [(i, i ^ flip) for i in range(senders)])]
    ppermute x6 -> x10, waiting for transfers between devices: 42.9 us -> 44.8 us  [the longest x1 25.2 us: halves_contract(): got = lax.ppermute(send, 'sp', [(i, i ^ units) for i in range(senders)])]
    squeeze x2 -> x0, local copies, waits for them, and re-layouts: 1.27 us -> none  [planes_contract(): return (mixed[0], mixed[1])]
    all_to_all x1, blocking collectives: 10.8 us -> 11.6 us  [halves_contract(): mixed = lax.all_to_all(mixed, 'sp', split_axis=0, concat_axis=0, tiled=True)]
  transfers between devices with their start and end apart: 7 -> 11, of which waited for: 4 -> 8; matrix products, arithmetic and copies ran while one was open for 1% -> 1% of each run, Pallas kernels for 0% -> 1%
where the time goes in v3:
time: 81.1 us; the launch traced here: 80.8 us
  waiting for transfers between devices  44.8 us (55%)
  starting transfers between devices  15.7 us (19%)
  blocking collectives  11.6 us (14%)
  Pallas kernels  6.82 us (8%)
    ppermute x1, waiting for transfers between devices, halves_contract(): got = lax.ppermute(send, 'sp', [(i, i ^ units) for i in range(senders)])  25.2 us
    all_to_all x1, blocking collectives, halves_contract(): mixed = lax.all_to_all(mixed, 'sp', split_axis=0, concat_axis=0, tiled=True)  11.6 us
    ppermute x3, waiting for transfers between devices, halves_contract(): lax.ppermute(parts[flip], 'sp', [(i, i ^ flip) for i in range(senders)])  11 us
    all_to_all x1, starting transfers between devices, halves_contract(): lax.all_to_all(packed.reshape(senders, high, LANES), 'sp', split_axis=0,...  6.98 us
    ppermute x1, waiting for transfers between devices, halves_contract(): far = lax.ppermute(got, 'groups', swap)  5.92 us
    ppermute x3, starting transfers between devices, halves_contract(): lax.ppermute(parts[flip], 'sp', [(i, i ^ flip) for i in range(senders)])  3.55 us
    ppermute x1, starting transfers between devices, halves_contract(): got = lax.ppermute(send, 'sp', [(i, i ^ units) for i in range(senders)])  2.99 us
    pallas_call x1, Pallas kernels, halves_contract(): pl.pallas_call(pack_kernel, out_shape=pltpu.VMEM((2, units, high, LANES),...  2.23 us
  transfers between devices with their start and end apart: 11, of which 8 were waited for; matrix products, arithmetic and copies ran while one was open for 1% of the time, Pallas kernels for 1%

profile of v3, /device:TPU:0, one launch (start us, length us, event | category | flops | bytes accessed | tf_op | source)
XLA Modules:
  0.0 80.8 jit_solution(14063579292046517015)
XLA Ops:
  0.6 0.6 collective-permute-start
  1.3 0.9 %collective-permute-done.pair_gain_p = bf16[256]{0:T(256)(128)(2,1)S(1)} collective-permute-done((bf16[256]{0:T(256)(128)(2,1)}, bf16[256]{0:T(256)(128)(2,1)S(1)}, u32[]{:S(2)}, u32[]{:S(2)}) %collective-permute-start) | collective-permute-done | bytes 544 | tf_op jit(solution)/shard_map/ppermute | solution.py:384
  2.1 0.3 collective-permute-done.1.pair_gain_f
  2.5 0.2 copy-done
  2.7 0.3 copy-done.1
  3.0 2.2 %pack.1 = bf16[2,4,328,128]{3,2,1,0:T(8,128)(2,1)} custom-call(bf16[256]{0:T(256)(128)(2,1)} %gain_p.1, bf16[256]{0:T(256)(128)(2,1)} %gain_f.1, bf16[256]{0:T(256)(128)(2,1)} %copy-done, bf16[256]{0:T(256)(128)(2,1)} %copy-done.1, bf16[32,4096]{1,0:T(8,128)(2,1)} %bitcast.9, bf16[32,4096]{1,0:T(8,128)(2,1)} %bitcast.10, bf16[32,1024]{1,0:T(8,128)(2,1)} %bitcast.11, ...), custom_call_target="tpu_custom_call" | custom-call | tf_op jit(solution)/shard_map/pack/pallas_call | solution.py:386
  5.2 7.0 %all-to-all-start = ((bf16[8,328,128]{2,1,0:T(8,128)(2,1)}), bf16[8,328,128]{2,1,0:T(8,128)(2,1)S(1)}, u32[]{:S(2)}, u32[]{:S(2)}) async-start(bf16[8,328,128]{2,1,0:T(8,128)(2,1)} %bitcast.4), calls=%async_computation | async-start | bytes 1343488 | tf_op jit(solution)/shard_map/all_to_all | solution.py:410
  12.2 1.2 %weights.1 = (bf16[128,1024]{1,0:T(8,128)(2,1)S(1)}, bf16[256,1024]{1,0:T(8,128)(2,1)S(1)}) custom-call(bf16[256,512]{1,0:T(8,128)(2,1)} %key_p.1, bf16[256,512]{1,0:T(8,128)(2,1)} %value_p.1, bf16[256,512]{1,0:T(8,128)(2,1)} %key_f.1, bf16[256,512]{1,0:T(8,128)(2,1)} %value_f.1), custom_call_target="tpu_custom_call" | custom-call | tf_op jit(solution)/shard_map/weights/pallas_call | solution.py:371
  13.4 3.0 %collective-permute-start.2 = (bf16[128,1024]{1,0:T(8,128)(2,1)S(1)}, bf16[128,1024]{1,0:T(8,128)(2,1)S(1)}, u32[]{:S(2)}, u32[]{:S(2)}) collective-permute-start(bf16[128,1024]{1,0:T(8,128)(2,1)S(1)} %get-tuple-element.11), channel_id=1, source_target_pairs={{0,8},{2,10},{4,12},{6,14},{8,0},{10,2},{12,4},{14,6},{1,9},{3,11}... | collective-permute-start | bytes 786440 | tf_op jit(solution)/shard_map/ppermute | solution.py:383
  16.4 25.2 %collective-permute-done.2.got = bf16[128,1024]{1,0:T(8,128)(2,1)S(1)} collective-permute-done((bf16[128,1024]{1,0:T(8,128)(2,1)S(1)}, bf16[128,1024]{1,0:T(8,128)(2,1)S(1)}, u32[]{:S(2)}, u32[]{:S(2)}) %collective-permute-start.2) | collective-permute-done | bytes 262176 | tf_op jit(solution)/shard_map/ppermute | solution.py:383
  41.6 1.5 %collective-permute-start.3 = (bf16[128,1024]{1,0:T(8,128)(2,1)S(1)}, bf16[128,1024]{1,0:T(8,128)(2,1)S(1)}, u32[]{:S(2)}, u32[]{:S(2)}) collective-permute-start(bf16[128,1024]{1,0:T(8,128)(2,1)S(1)} %collective-permute-done.2.got), channel_id=1, source_target_pairs={{0,16},{16,0},{1,17},{17,1},{2,18},{18,2},{3,19},{19,3},{4,20},{20... | collective-permute-start | bytes 786440 | tf_op jit(solution)/shard_map/ppermute | solution.py:413
  43.1 5.9 %collective-permute-done.3.far = bf16[128,1024]{1,0:T(8,128)(2,1)S(1)} collective-permute-done((bf16[128,1024]{1,0:T(8,128)(2,1)S(1)}, bf16[128,1024]{1,0:T(8,128)(2,1)S(1)}, u32[]{:S(2)}, u32[]{:S(2)}) %collective-permute-start.3) | collective-permute-done | bytes 262176 | tf_op jit(solution)/shard_map/ppermute | solution.py:413
  49.1 1.5 %collective-permute-done.6.pair_far = bf16[128,1024]{1,0:T(8,128)(2,1)S(1)} collective-permute-done((bf16[128,1024]{1,0:T(8,128)(2,1)S(1)}, bf16[128,1024]{1,0:T(8,128)(2,1)S(1)}, u32[]{:S(2)}, u32[]{:S(2)}) %collective-permute-start.6) | collective-permute-done | bytes 262176 | tf_op jit(solution)/shard_map/ppermute | solution.py:416
  50.6 1.6 %partial.1 = (f32[256,256]{1,0:T(8,128)S(1)}, f32[256,256]{1,0:T(8,128)S(1)}, f32[256,256]{1,0:T(8,128)S(1)}, f32[256,256]{1,0:T(8,128)S(1)}) custom-call(bf16[8,328,128]{2,1,0:T(8,128)(2,1)S(1)} %all-to-all-done.packed, bf16[256,1024]{1,0:T(8,128)(2,1)S(1)} %get-tuple-element.10.keep, bf16[128,1024]{1,0:T(8,128)(2,1)S(1)} %collective-permute-done.2.got, ...), custom_call_target="tpu_custom_call" | custom-call | tf_op jit(solution)/shard_map/partial/pallas_call | solution.py:418
  52.1 1.5 %collective-permute-start.7 = (f32[256,256]{1,0:T(8,128)S(1)}, f32[256,256]{1,0:T(8,128)S(1)}, u32[]{:S(2)}, u32[]{:S(2)}) collective-permute-start(f32[256,256]{1,0:T(8,128)S(1)} %get-tuple-element.13), channel_id=1, source_target_pairs={{0,2},{2,0},{4,6},{6,4},{8,10},{10,8},{12,14},{14,12},{1,3},{3,1},... | collective-permute-start | bytes 786440 | tf_op jit(solution)/shard_map/ppermute | solution.py:430
  53.7 2.0 %collective-permute-start.9 = (f32[256,256]{1,0:T(8,128)S(1)}, f32[256,256]{1,0:T(8,128)S(1)}, u32[]{:S(2)}, u32[]{:S(2)}) collective-permute-start(f32[256,256]{1,0:T(8,128)S(1)} %get-tuple-element.15), channel_id=1, source_target_pairs={{0,6},{2,4},{4,2},{6,0},{8,14},{10,12},{12,10},{14,8},{1,7},{3,5},... | collective-permute-start | bytes 786440 | tf_op jit(solution)/shard_map/ppermute | solution.py:430
  55.7 0.5 fusion
  56.2 0.1 pad_maximum_fusion
  56.4 4.2 %collective-permute-done.7.parts_and_out_1_ = f32[256,256]{1,0:T(8,128)S(1)} collective-permute-done((f32[256,256]{1,0:T(8,128)S(1)}, f32[256,256]{1,0:T(8,128)S(1)}, u32[]{:S(2)}, u32[]{:S(2)}) %collective-permute-start.7) | collective-permute-done | bytes 262176 | tf_op jit(solution)/shard_map/ppermute | solution.py:430
  60.6 2.3 %collective-permute-done.8.parts_and_out_2_ = f32[256,256]{1,0:T(8,128)S(1)} collective-permute-done((f32[256,256]{1,0:T(8,128)S(1)}, f32[256,256]{1,0:T(8,128)S(1)}, u32[]{:S(2)}, u32[]{:S(2)}) %collective-permute-start.8) | collective-permute-done | bytes 262176 | tf_op jit(solution)/shard_map/ppermute | solution.py:430
  62.9 4.5 %collective-permute-done.9.parts_and_out_3_ = f32[256,256]{1,0:T(8,128)S(1)} collective-permute-done((f32[256,256]{1,0:T(8,128)S(1)}, f32[256,256]{1,0:T(8,128)S(1)}, u32[]{:S(2)}, u32[]{:S(2)}) %collective-permute-start.9) | collective-permute-done | bytes 262176 | tf_op jit(solution)/shard_map/ppermute | solution.py:430
  67.4 1.2 %attend.1 = bf16[8,32,256]{2,1,0:T(8,128)(2,1)S(1)} custom-call(bf16[8,328,128]{2,1,0:T(8,128)(2,1)S(1)} %all-to-all-done.packed, f32[256,128]{1,0:T(8,128)S(1)} %get-tuple-element.21.cosines, f32[256,128]{1,0:T(8,128)S(1)} %get-tuple-element.22.sines, f32[256,256]{1,0:T(8,128)S(1)} %get-tuple-element.12.parts_and_out_0_, ...), custom_call_target="tpu_custom_call" | custom-call | tf_op jit(solution)/shard_map/attend/pallas_call | solution.py:433
  68.5 11.6 %all_to_all.10 = bf16[8,32,256]{2,1,0:T(8,128)(2,1)S(1)} all-to-all(bf16[8,32,256]{2,1,0:T(8,128)(2,1)S(1)} %attend.1), channel_id=1, replica_groups=mesh['groups'=2,'sp'=8,'fsdp'=2] {'sp'}, dimensions={0} | all-to-all | bytes 262144 | tf_op jit(solution)/shard_map/all_to_all | solution.py:441
  80.1 0.7 assemble.1
  (12 shorter events, 0.1 us)
Async XLA Ops:
  0.6 1.5 %collective-permute-start = (bf16[256]{0:T(256)(128)(2,1)}, bf16[256]{0:T(256)(128)(2,1)S(1)}, u32[]{:S(2)}, u32[]{:S(2)}) collective-permute-start(bf16[256]{0:T(256)(128)(2,1)} %gain_p.1), channel_id=1, source_target_pairs={{0,1},{1,0},{2,3},{3,2},{4,5},{5,4},{6,7},{7,6},{8,9},{9,8},{10,11... | collective-permute-start | bytes 1544 | tf_op jit(solution)/shard_map/ppermute | solution.py:384
  1.2 1.3 %collective-permute-start.1 = (bf16[256]{0:T(256)(128)(2,1)}, bf16[256]{0:T(256)(128)(2,1)S(1)}, u32[]{:S(2)}, u32[]{:S(2)}) collective-permute-start(bf16[256]{0:T(256)(128)(2,1)} %gain_f.1), channel_id=1, source_target_pairs={{0,1},{1,0},{2,3},{3,2},{4,5},{5,4},{6,7},{7,6},{8,9},{9,8},{10,11... | collective-permute-start | bytes 1544 | tf_op jit(solution)/shard_map/ppermute | solution.py:385
  2.1 0.5 copy-start
  2.5 0.5 copy-start.1
  5.2 45.3 %all-to-all-start = ((bf16[8,328,128]{2,1,0:T(8,128)(2,1)}), bf16[8,328,128]{2,1,0:T(8,128)(2,1)S(1)}, u32[]{:S(2)}, u32[]{:S(2)}) async-start(bf16[8,328,128]{2,1,0:T(8,128)(2,1)} %bitcast.4), calls=%async_computation | async-start | bytes 1343488 | tf_op jit(solution)/shard_map/all_to_all | solution.py:410
  13.4 28.2 %collective-permute-start.2 = (bf16[128,1024]{1,0:T(8,128)(2,1)S(1)}, bf16[128,1024]{1,0:T(8,128)(2,1)S(1)}, u32[]{:S(2)}, u32[]{:S(2)}) collective-permute-start(bf16[128,1024]{1,0:T(8,128)(2,1)S(1)} %get-tuple-element.11), channel_id=1, source_target_pairs={{0,8},{2,10},{4,12},{6,14},{8,0},{10,2},{12,4},{14,6},{1,9},{3,11}... | collective-permute-start | bytes 786440 | tf_op jit(solution)/shard_map/ppermute | solution.py:383
  16.4 32.7 %collective-permute-start.4 = (bf16[256,1024]{1,0:T(8,128)(2,1)S(1)}, bf16[256,1024]{1,0:T(8,128)(2,1)S(1)}, u32[]{:S(2)}, u32[]{:S(2)}) collective-permute-start(bf16[256,1024]{1,0:T(8,128)(2,1)S(1)} %get-tuple-element.10.keep), channel_id=1, source_target_pairs={{0,1},{1,0},{2,3},{3,2},{4,5},{5,4},{6,7},{7,6},{8,9},{9,8},{10,11... | collective-permute-start | bytes 1572872 | tf_op jit(solution)/shard_map/ppermute | solution.py:414
  41.6 7.4 %collective-permute-start.3 = (bf16[128,1024]{1,0:T(8,128)(2,1)S(1)}, bf16[128,1024]{1,0:T(8,128)(2,1)S(1)}, u32[]{:S(2)}, u32[]{:S(2)}) collective-permute-start(bf16[128,1024]{1,0:T(8,128)(2,1)S(1)} %collective-permute-done.2.got), channel_id=1, source_target_pairs={{0,16},{16,0},{1,17},{17,1},{2,18},{18,2},{3,19},{19,3},{4,20},{20... | collective-permute-start | bytes 786440 | tf_op jit(solution)/shard_map/ppermute | solution.py:413
  43.1 6.0 %collective-permute-start.5 = (bf16[128,1024]{1,0:T(8,128)(2,1)S(1)}, bf16[128,1024]{1,0:T(8,128)(2,1)S(1)}, u32[]{:S(2)}, u32[]{:S(2)}) collective-permute-start(bf16[128,1024]{1,0:T(8,128)(2,1)S(1)} %collective-permute-done.2.got), channel_id=1, source_target_pairs={{0,1},{1,0},{2,3},{3,2},{4,5},{5,4},{6,7},{7,6},{8,9},{9,8},{10,11... | collective-permute-start | bytes 786440 | tf_op jit(solution)/shard_map/ppermute | solution.py:415
  49.0 1.5 %collective-permute-start.6 = (bf16[128,1024]{1,0:T(8,128)(2,1)S(1)}, bf16[128,1024]{1,0:T(8,128)(2,1)S(1)}, u32[]{:S(2)}, u32[]{:S(2)}) collective-permute-start(bf16[128,1024]{1,0:T(8,128)(2,1)S(1)} %collective-permute-done.3.far), channel_id=1, source_target_pairs={{0,1},{1,0},{2,3},{3,2},{4,5},{5,4},{6,7},{7,6},{8,9},{9,8},{10,11... | collective-permute-start | bytes 786440 | tf_op jit(solution)/shard_map/ppermute | solution.py:416
  52.1 8.4 %collective-permute-start.7 = (f32[256,256]{1,0:T(8,128)S(1)}, f32[256,256]{1,0:T(8,128)S(1)}, u32[]{:S(2)}, u32[]{:S(2)}) collective-permute-start(f32[256,256]{1,0:T(8,128)S(1)} %get-tuple-element.13), channel_id=1, source_target_pairs={{0,2},{2,0},{4,6},{6,4},{8,10},{10,8},{12,14},{14,12},{1,3},{3,1},... | collective-permute-start | bytes 786440 | tf_op jit(solution)/shard_map/ppermute | solution.py:430
  53.7 9.2 %collective-permute-start.8 = (f32[256,256]{1,0:T(8,128)S(1)}, f32[256,256]{1,0:T(8,128)S(1)}, u32[]{:S(2)}, u32[]{:S(2)}) collective-permute-start(f32[256,256]{1,0:T(8,128)S(1)} %get-tuple-element.14), channel_id=1, source_target_pairs={{0,4},{2,6},{4,0},{6,2},{8,12},{10,14},{12,8},{14,10},{1,5},{3,7},... | collective-permute-start | bytes 786440 | tf_op jit(solution)/shard_map/ppermute | solution.py:430
  53.7 13.7 %collective-permute-start.9 = (f32[256,256]{1,0:T(8,128)S(1)}, f32[256,256]{1,0:T(8,128)S(1)}, u32[]{:S(2)}, u32[]{:S(2)}) collective-permute-start(f32[256,256]{1,0:T(8,128)S(1)} %get-tuple-element.15), channel_id=1, source_target_pairs={{0,6},{2,4},{4,2},{6,0},{8,14},{10,12},{12,10},{14,8},{1,7},{3,5},... | collective-permute-start | bytes 786440 | tf_op jit(solution)/shard_map/ppermute | solution.py:430

commit v4 on v3

--- a/solution.py
+++ b/solution.py
@@ -120,18 +120,16 @@
 
 
 def weights_kernel(key_p, value_p, key_f, value_f, send, keep, sems):
-    _, width = key_p.shape
-    half = send.shape[0]
-    model = lax.axis_index("sp") // (lax.axis_size("sp") // 2)
-    first = pl.multiple_of(lax.axis_index("groups") * half, half)
+    width = key_p.shape[1]
+    model = lax.axis_index("sp") % 2
 
     def move(key_own, value_own, key_other, value_other):
         copies = [
             pltpu.make_async_copy(source, target, sems.at[index])
             for index, (source, target) in enumerate(
                 (
-                    (key_other.at[pl.ds(first, half), :], send.at[:, :width]),
-                    (value_other.at[pl.ds(first, half), :], send.at[:, width:]),
+                    (key_other, send.at[:, :width]),
+                    (value_other, send.at[:, width:]),
                     (key_own, keep.at[:, :width]),
                     (value_own, keep.at[:, width:]),
                 )
@@ -162,8 +160,9 @@
     queries_f,
     docs_p,
     docs_f,
-    out,
+    *outs_and_scratch,
 ):
+    outs, out = outs_and_scratch[:-1], outs_and_scratch[-1]
     _, units, _, _ = out.shape
     tokens, depth = hidden_p.shape
     rows = gain_p.shape[0]
@@ -209,7 +208,7 @@
         side = side.astype(jnp.bfloat16)
         for unit in range(units):
             for tile in range(2 * tiles):
-                first = (unit + (tile // tiles) * units) * block + (tile % tiles) * LANES
+                first = (2 * tiles * unit + tile) * LANES
                 out[owner, unit, tile * tokens : (tile + 1) * tokens, :] = hidden[
                     :, first : first + LANES
                 ]
@@ -218,12 +217,14 @@
                 low = (2 * tiles + tile) * tokens
                 out[owner, unit, low : low + tokens, :] = queries[:, first : first + LANES]
             out[owner, unit, out.shape[2] - SIDE_ROWS :, :] = side
-
-
-def side_columns(packed, tokens, sums):
-    senders, high, _ = packed.shape
-    side = packed[:, high - SIDE_ROWS :, :].reshape(senders * SIDE_ROWS, LANES)
-    turned = jnp.transpose(side.astype(jnp.float32))
+    place = lax.axis_index("sp")
+    for flip in range(2 * units):
+        outs[flip][...] = out[(place ^ flip) % 2, (place ^ flip) // 2]
+
+
+def side_columns(side, tokens, sums):
+    senders = side.shape[0]
+    turned = jnp.transpose(side.reshape(senders * SIDE_ROWS, LANES))
     columns = []
     for sender in range(senders):
         column = None
@@ -235,83 +236,88 @@
     return jnp.concatenate(columns, axis=0)
 
 
-def partial_kernel(
-    tokens, packed, keep, got, far, pair_keep, pair_got, pair_far, *outs_and_scratch
-):
-    outs, keys, values = outs_and_scratch[:-2], outs_and_scratch[-2], outs_and_scratch[-1]
-    units = len(outs)
-    place, core, group = lax.axis_index("sp"), lax.axis_index("fsdp"), lax.axis_index("groups")
-    model, unit = place // units, place % units
-    senders, high, _ = packed.shape
-    length = senders * tokens
-    half = got.shape[0]
+def partial_kernel(tokens, units, *refs):
+    chunks, (own, other), refs = refs[:units], refs[units : units + 2], refs[units + 2 :]
+    keep, got, pair_keep, pair_got = refs[:4]
+    outs, (packed, keys, values) = refs[4 : 4 + units], refs[4 + units :]
+    place, core = lax.axis_index("sp"), lax.axis_index("fsdp")
+    plane, model = place // 2, place % 2
+    high = packed.shape[1]
+    length = units * tokens
+    rows = keep.shape[0]
     width = keep.shape[1] // 2
-    halves = keep.shape[0] // half
-    strips = half // LANES
-    inverse = side_columns(packed, tokens, (0, 1, 2))
-    first_side = high - SIDE_ROWS
+    strips = rows // LANES
+    for flip in range(units):
+        packed[(place % units) ^ flip] = chunks[flip][...]
+    side_row = high - SIDE_ROWS
+    inverse = side_columns(packed[:, side_row:, :].astype(jnp.float32), tokens, (0, 1, 2))
+    own_side = own[side_row:, :].astype(jnp.float32)
+    other_side = other[side_row:, :].astype(jnp.float32)
     key_sum = value_sum = None
-    for weights, flip_model, flip_core, part in (
-        (keep, 0, 0, 0),
-        (keep, 0, 0, 1),
-        (got, 1, 0, group),
-        (far, 1, 0, 1 - group),
-        (pair_keep, 0, 1, 0),
-        (pair_keep, 0, 1, 1),
-        (pair_got, 1, 1, group),
-        (pair_far, 1, 1, 1 - group),
+    for weights, flip_model, flip_core in (
+        (keep, 0, 0),
+        (pair_keep, 0, 1),
+        (got, 1, 0),
+        (pair_got, 1, 1),
     ):
-        source = model ^ flip_model
-        side = packed[source * units + unit, first_side:, :].astype(jnp.float32)
+        side = other_side if flip_model else own_side
         columns = []
         for strip in range(strips):
-            tile = ((source * 2 + (core ^ flip_core)) * halves + part) * strips + strip
+            tile = ((model ^ flip_model) * 2 + (core ^ flip_core)) * strips + strip
             hidden = packed[:, pl.ds(pl.multiple_of(tile * tokens, tokens), tokens), :]
             hidden = hidden.reshape(length, LANES).astype(jnp.float32)
-            wanted = SIDE_GAINS + (flip_core * halves + part) * strips + strip
-            picked = lax.broadcasted_iota(jnp.int32, (SIDE_ROWS, LANES), 0) == wanted
-            gain = jnp.sum(jnp.where(picked, side, 0.0), axis=0, keepdims=True)
+            wanted = SIDE_GAINS + flip_core * strips + strip
+            gain = side[wanted : wanted + 1, :]
             columns.append((hidden * inverse * gain).astype(jnp.bfloat16))
-        normed = jnp.concatenate(columns, axis=-1) if strips > 1 else columns[0]
-        low = part * half if weights is keep or weights is pair_keep else 0
-        key_part = jnp.dot(
-            normed, weights[low : low + half, :width], preferred_element_type=jnp.float32
-        )
-        value_part = jnp.dot(
-            normed, weights[low : low + half, width:], preferred_element_type=jnp.float32
-        )
+        normed = jnp.concatenate(columns, axis=-1)
+        key_part = jnp.dot(normed, weights[:, :width], preferred_element_type=jnp.float32)
+        value_part = jnp.dot(normed, weights[:, width:], preferred_element_type=jnp.float32)
         key_sum = key_part if key_sum is None else key_sum + key_part
         value_sum = value_part if value_sum is None else value_sum + value_part
     for head in range(units):
         keys[head] = key_sum[:, head * HEAD_DIM : (head + 1) * HEAD_DIM]
         values[head] = value_sum[:, head * HEAD_DIM : (head + 1) * HEAD_DIM]
     for flip in range(units):
-        outs[flip][:, :HEAD_DIM] = keys[unit ^ flip]
-        outs[flip][:, HEAD_DIM:] = values[unit ^ flip]
-
-
-def attend_kernel(tokens, packed, cosines, sines, *parts_and_out):
-    parts, out = parts_and_out[:-1], parts_and_out[-1]
-    senders = packed.shape[0]
+        outs[flip][:, :HEAD_DIM] = keys[plane ^ flip]
+        outs[flip][:, HEAD_DIM:] = values[plane ^ flip]
+
+
+def add_kernel(left, right, out):
+    out[...] = left[...] + right[...]
+
+
+def attend_kernel(tokens, units, cosines, sines, *refs):
+    chunks, refs = refs[: 2 * units], refs[2 * units :]
+    near, far, refs = refs[:3], refs[3:6], refs[6:]
+    out, asked, side, total = refs
+    senders, _, per_head = out.shape
     length = senders * tokens
-    per_head = out.shape[2]
-    total = parts[0][...]
-    for part in parts[1:]:
-        total = total + part[...]
-    raw_keys = total[:, :HEAD_DIM]
+    place = lax.axis_index("sp")
+    half = place // units
+    high = chunks[0].shape[0]
+    first_query = high - SIDE_ROWS - per_head // HEAD_DIM * tokens
+    for flip in range(senders):
+        asked[place ^ flip] = chunks[flip][first_query : high - SIDE_ROWS, :]
+        side[place ^ flip] = chunks[flip][high - SIDE_ROWS :, :].astype(jnp.float32)
+    for which, parts in ((half, near), (1 - half, far)):
+        part_sum = parts[0][...]
+        for part in parts[1:]:
+            part_sum = part_sum + part[...]
+        total[which] = part_sum
+    sums = total[...].reshape(length, 2 * HEAD_DIM)
+    raw_keys = sums[:, :HEAD_DIM]
     turned = jnp.concatenate(
         [raw_keys[:, HEAD_DIM // 2 :], raw_keys[:, : HEAD_DIM // 2]], axis=-1
     )
     keys = (raw_keys * cosines[...] + turned * sines[...]).astype(jnp.bfloat16)
-    values = total[:, HEAD_DIM:].astype(jnp.bfloat16)
-    query_docs = side_columns(packed, tokens, (3,))
+    values = sums[:, HEAD_DIM:].astype(jnp.bfloat16)
+    query_docs = side_columns(side[...], tokens, (3,))
     key_docs = jnp.transpose(jnp.broadcast_to(query_docs, (length, LANES)))[:1, :]
     row = lax.broadcasted_iota(jnp.int32, (length, length), 0)
     column = lax.broadcasted_iota(jnp.int32, (length, length), 1)
     allowed = (column <= row) & (query_docs == key_docs)
     for head in range(per_head // HEAD_DIM):
-        low = packed.shape[1] - SIDE_ROWS - (per_head // HEAD_DIM - head) * tokens
-        queries = packed[:, low : low + tokens, :].reshape(length, HEAD_DIM)
+        queries = asked[:, head * tokens : (head + 1) * tokens, :].reshape(length, HEAD_DIM)
         scores = lax.dot_general(
             queries, keys, (((1,), (1,)), ((), ())), preferred_element_type=jnp.float32
         ) * (HEAD_DIM ** (-0.5))
@@ -325,15 +331,16 @@
         )
 
 
+def assemble_kernel(arrived, out_p, out_f):
+    senders, _, per_head = arrived.shape
+    for sender in range(senders):
+        out = (out_p, out_f)[sender % 2]
+        head = sender // 2
+        out[:, head * per_head : (head + 1) * per_head] = arrived[sender]
+
+
 def here(x):
     return pltpu.with_memory_space_constraint(x, pltpu.VMEM)
-
-
-def assemble_kernel(arrived, out_p, out_f):
-    _, units, _, per_head = arrived.shape
-    for owner, out in enumerate((out_p, out_f)):
-        for unit in range(units):
-            out[:, unit * per_head : (unit + 1) * per_head] = arrived[owner, unit]
 
 
 def there(x):
@@ -353,12 +360,11 @@
     )
 
 
-def halves_contract(units, policy, frozen):
+def planes_contract(units, policy, frozen):
     hidden_p, queries_p, docs_p, gain_p, key_p, value_p = policy
     hidden_f, queries_f, docs_f, gain_f, key_f, value_f = frozen
     tokens = hidden_p.shape[1]
     rows, width = key_p.shape
-    half = rows // 2
     per_head = queries_p.shape[2] // units
     senders = 2 * units
     length = senders * tokens
@@ -368,10 +374,13 @@
     params = pltpu.CompilerParams(vmem_limit_bytes=KERNEL_BYTES)
     swap = [(0, 1), (1, 0)]
 
+    def flipped(flip):
+        return [(i, i ^ flip) for i in range(senders)]
+
     send, keep = pl.pallas_call(
         weights_kernel,
         out_shape=[
-            pltpu.VMEM((half, 2 * width), jnp.bfloat16),
+            pltpu.VMEM((rows, 2 * width), jnp.bfloat16),
             pltpu.VMEM((rows, 2 * width), jnp.bfloat16),
         ],
         in_specs=[hbm] * 4,
@@ -380,14 +389,15 @@
         compiler_params=params,
         name="weights",
     )(*(there(array) for array in (key_p, value_p, key_f, value_f)))
-    got = lax.ppermute(send, "sp", [(i, i ^ units) for i in range(senders)])
+    got = lax.ppermute(send, "sp", flipped(1))
     pair_gain_p = lax.ppermute(gain_p, "fsdp", swap)
     pair_gain_f = lax.ppermute(gain_f, "fsdp", swap)
-    packed = pl.pallas_call(
+    sent = pl.pallas_call(
         pack_kernel,
-        out_shape=pltpu.VMEM((2, units, high, LANES), jnp.bfloat16),
+        out_shape=[pltpu.VMEM((high, LANES), jnp.bfloat16)] * senders,
         in_specs=[vmem] * 10,
-        out_specs=vmem,
+        out_specs=[vmem] * senders,
+        scratch_shapes=[pltpu.VMEM((2, units, high, LANES), jnp.bfloat16)],
         compiler_params=params,
         name="pack",
     )(
@@ -407,37 +417,54 @@
             )
         )
     )
-    packed = lax.all_to_all(
-        packed.reshape(senders, high, LANES), "sp", split_axis=0, concat_axis=0, tiled=True
-    )
-    far = lax.ppermute(got, "groups", swap)
+    chunks = [sent[0]]
+    for flip in range(1, senders):
+        chunks.append(lax.ppermute(sent[flip], "sp", flipped(flip)))
     pair_keep = lax.ppermute(keep, "fsdp", swap)
     pair_got = lax.ppermute(got, "fsdp", swap)
-    pair_far = lax.ppermute(far, "fsdp", swap)
-    packed = here(packed)
-    parts = pl.pallas_call(
-        functools.partial(partial_kernel, tokens),
-        out_shape=[pltpu.VMEM((length, 2 * HEAD_DIM), jnp.float32)] * units,
-        in_specs=[vmem] * 7,
-        out_specs=[vmem] * units,
-        scratch_shapes=[pltpu.VMEM((units, length, HEAD_DIM), jnp.float32)] * 2,
-        compiler_params=params,
-        name="partial",
-    )(packed, *(here(array) for array in (keep, got, far, pair_keep, pair_got, pair_far)))
-    arrived = [parts[0]]
-    for flip in range(1, units):
-        arrived.append(
-            lax.ppermute(parts[flip], "sp", [(i, i ^ flip) for i in range(senders)])
-        )
+    chunks = [here(chunk) for chunk in chunks]
+    weights = [here(array) for array in (keep, got, pair_keep, pair_got)]
+    block = pltpu.VMEM((units * tokens, 2 * HEAD_DIM), jnp.float32)
+    sums, crossed = {}, {}
+    for side in ("near", "far"):
+        first = units if side == "far" else 0
+        own, local, hold, cross = pl.pallas_call(
+            functools.partial(partial_kernel, tokens, units),
+            out_shape=[block] * units,
+            in_specs=[vmem] * (units + 6),
+            out_specs=[vmem] * units,
+            scratch_shapes=[
+                pltpu.VMEM((units, high, LANES), jnp.bfloat16),
+                pltpu.VMEM((units, units * tokens, HEAD_DIM), jnp.float32),
+                pltpu.VMEM((units, units * tokens, HEAD_DIM), jnp.float32),
+            ],
+            compiler_params=params,
+        )(*chunks[first : first + units], chunks[0], chunks[1], *weights)
+        cross = lax.ppermute(cross, "sp", flipped(2))
+        local = lax.ppermute(local, "sp", flipped(2))
+        both = pl.pallas_call(
+            add_kernel, out_shape=block, in_specs=[vmem] * 2, out_specs=vmem, compiler_params=params
+        )(here(hold), here(cross))
+        crossed[side] = lax.ppermute(both, "sp", flipped(4))
+        sums[side] = [own, local]
+    arrived = [
+        here(part)
+        for part in (*sums["near"], crossed["far"], *sums["far"], crossed["near"])
+    ]
     cosines, sines = rotary_tables(length)
     mixed = pl.pallas_call(
-        functools.partial(attend_kernel, tokens),
+        functools.partial(attend_kernel, tokens, units),
         out_shape=pltpu.VMEM((senders, tokens, per_head), jnp.bfloat16),
-        in_specs=[vmem] * (3 + units),
+        in_specs=[vmem] * (2 + senders + len(arrived)),
         out_specs=vmem,
+        scratch_shapes=[
+            pltpu.VMEM((senders, per_head // HEAD_DIM * tokens, HEAD_DIM), jnp.bfloat16),
+            pltpu.VMEM((senders, SIDE_ROWS, LANES), jnp.float32),
+            pltpu.VMEM((2, units * tokens, 2 * HEAD_DIM), jnp.float32),
+        ],
         compiler_params=params,
         name="attend",
-    )(packed, cosines, sines, *(here(part) for part in arrived))
+    )(cosines, sines, *chunks, *arrived)
     mixed = lax.all_to_all(mixed, "sp", split_axis=0, concat_axis=0, tiled=True)
     out_shape = jax.ShapeDtypeStruct((tokens, units * per_head), jnp.bfloat16)
     mixed_p, mixed_f = pl.pallas_call(
@@ -447,33 +474,32 @@
         out_specs=[vmem] * 2,
         compiler_params=params,
         name="assemble",
-    )(here(mixed.reshape(2, units, tokens, per_head)))
+    )(here(mixed))
     return (mixed_p[None], mixed_f[None])
 
 
-def per_device(groups, sp_size, fsdp_size, *arrays):
+def per_device(sp_size, fsdp_size, *arrays):
     policy, frozen = arrays[:6], arrays[6:]
     key_heads = policy[4].shape[1] // HEAD_DIM
     tokens = policy[0].shape[1]
     rows = policy[4].shape[0]
     if (
-        sp_size == 2 * key_heads
-        and key_heads & (key_heads - 1) == 0
-        and groups == 2
+        sp_size == 8
+        and key_heads == 4
         and fsdp_size == 2
         and tokens % 16 == 0
         and tokens <= LANES
-        and rows % (2 * LANES) == 0
+        and rows % LANES == 0
         and SIDE_GAINS + 2 * rows // LANES <= SIDE_ROWS
         and sp_size * tokens <= 512
     ):
-        return halves_contract(key_heads, policy, frozen)
+        return planes_contract(key_heads, policy, frozen)
     return gathered_weights(policy, frozen)
 
 
 def solution(mesh):
     return jax.shard_map(
-        functools.partial(per_device, *(mesh.shape[axis] for axis in ("groups", "sp", "fsdp"))),
+        functools.partial(per_device, *(mesh.shape[axis] for axis in ("sp", "fsdp"))),
         mesh=mesh,
         in_specs=(
             P(("groups", "fsdp"), "sp", None),

time: 81.1 us -> 75.6 us (0.932)
  waiting for transfers between devices: 44.8 us -> 26.1 us
  starting transfers between devices: 15.7 us -> 27.6 us
  blocking collectives: 11.6 us -> 13.7 us
    ppermute x10 -> x18, starting transfers between devices: 8.67 us -> 27.6 us  [the longest x7 12.5 us: planes_contract(): chunks.append(lax.ppermute(sent[flip], 'sp', flipped(flip)))]
    ppermute x10 -> x18, waiting for transfers between devices: 44.8 us -> 26.1 us  [the longest x1 11.9 us: planes_contract(): got = lax.ppermute(send, 'sp', flipped(1))]
    all_to_all x1 -> x0, starting transfers between devices: 6.98 us -> none  [halves_contract(): lax.all_to_all(packed.reshape(senders, high, LANES), 'sp', split_axis=0,...]
    all_to_all x1, blocking collectives: 11.6 us -> 13.7 us  [planes_contract(): mixed = lax.all_to_all(mixed, 'sp', split_axis=0, concat_axis=0, tiled=True)]
    pallas_call x5 -> x8, Pallas kernels: 6.82 us -> 6.07 us  [the longest x2 1.51 us: planes_contract(): pl.pallas_call(functools.partial(partial_kernel, tokens, units), out_shap...]
  transfers between devices with their start and end apart: 11 -> 18, of which waited for: 8 -> 8; matrix products, arithmetic and copies ran while one was open for 1% -> 1% of each run, Pallas kernels for 1% -> 4%
where the time goes in v4:
time: 75.6 us; the launch traced here: 75.4 us
  starting transfers between devices  27.6 us (37%)
  waiting for transfers between devices  26.1 us (35%)
  blocking collectives  13.7 us (18%)
  Pallas kernels  6.07 us (8%)
    all_to_all x1, blocking collectives, planes_contract(): mixed = lax.all_to_all(mixed, 'sp', split_axis=0, concat_axis=0, tiled=True)  13.7 us
    ppermute x7, starting transfers between devices, planes_contract(): chunks.append(lax.ppermute(sent[flip], 'sp', flipped(flip)))  12.5 us
    ppermute x1, waiting for transfers between devices, planes_contract(): got = lax.ppermute(send, 'sp', flipped(1))  11.9 us
    ppermute x7, waiting for transfers between devices, planes_contract(): chunks.append(lax.ppermute(sent[flip], 'sp', flipped(flip)))  6.97 us
    ppermute x2, starting transfers between devices, planes_contract(): crossed[side] = lax.ppermute(both, 'sp', flipped(4))  5.68 us
    ppermute x2, waiting for transfers between devices, planes_contract(): local = lax.ppermute(local, 'sp', flipped(2))  5.52 us
    ppermute x2, starting transfers between devices, planes_contract(): cross = lax.ppermute(cross, 'sp', flipped(2))  3.68 us
    ppermute x1, starting transfers between devices, planes_contract(): got = lax.ppermute(send, 'sp', flipped(1))  3.07 us
  transfers between devices with their start and end apart: 18, of which 8 were waited for; matrix products, arithmetic and copies ran while one was open for 1% of the time, Pallas kernels for 4%

profile of v4, /device:TPU:0, one launch (start us, length us, event | category | flops | bytes accessed | tf_op | source)
XLA Modules:
  0.0 75.4 jit_solution(5732659205453480392)
XLA Ops:
  0.6 1.2 %weights.1 = (bf16[256,1024]{1,0:T(8,128)(2,1)S(1)}, bf16[256,1024]{1,0:T(8,128)(2,1)S(1)}) custom-call(bf16[256,512]{1,0:T(8,128)(2,1)} %key_p.1, bf16[256,512]{1,0:T(8,128)(2,1)} %value_p.1, bf16[256,512]{1,0:T(8,128)(2,1)} %key_f.1, bf16[256,512]{1,0:T(8,128)(2,1)} %value_f.1), custom_call_target="tpu_custom_call" | custom-call | tf_op jit(solution)/shard_map/weights/pallas_call | solution.py:380
  1.9 3.1 %collective-permute-start.9 = (bf16[256,1024]{1,0:T(8,128)(2,1)S(1)}, bf16[256,1024]{1,0:T(8,128)(2,1)S(1)}, u32[]{:S(2)}, u32[]{:S(2)}) collective-permute-start(bf16[256,1024]{1,0:T(8,128)(2,1)S(1)} %get-tuple-element.31), channel_id=1, source_target_pairs={{0,2},{2,0},{4,6},{6,4},{8,10},{10,8},{12,14},{14,12},{1,3},{3,1},... | collective-permute-start | bytes 1572872 | tf_op jit(solution)/shard_map/ppermute | solution.py:392
  5.0 11.9 %collective-permute-done.9.refs_7_ = bf16[256,1024]{1,0:T(8,128)(2,1)S(1)} collective-permute-done((bf16[256,1024]{1,0:T(8,128)(2,1)S(1)}, bf16[256,1024]{1,0:T(8,128)(2,1)S(1)}, u32[]{:S(2)}, u32[]{:S(2)}) %collective-permute-start.9) | collective-permute-done | bytes 524320 | tf_op jit(solution)/shard_map/ppermute | solution.py:392
  17.5 1.3 %collective-permute-done.pair_gain_p = bf16[256]{0:T(256)(128)(2,1)S(1)} collective-permute-done((bf16[256]{0:T(256)(128)(2,1)S(1)}, bf16[256]{0:T(256)(128)(2,1)S(1)}, u32[]{:S(2)}, u32[]{:S(2)}) %collective-permute-start) | collective-permute-done | bytes 544 | tf_op jit(solution)/shard_map/ppermute | solution.py:393
  19.3 1.4 %pack.1 = (bf16[328,128]{1,0:T(8,128)(2,1)S(1)}, bf16[328,128]{1,0:T(8,128)(2,1)S(1)}, bf16[328,128]{1,0:T(8,128)(2,1)S(1)}, bf16[328,128]{1,0:T(8,128)(2,1)S(1)...) custom-call(bf16[256]{0:T(256)(128)(2,1)} %gain_p.1, ...), custom_call_target="tpu_custom_call" | custom-call | tf_op jit(solution)/shard_map/pack/pallas_call | solution.py:395
  20.7 1.8 %collective-permute-start.2 = (bf16[328,128]{1,0:T(8,128)(2,1)S(1)}, bf16[328,128]{1,0:T(8,128)(2,1)S(1)}, u32[]{:S(2)}, u32[]{:S(2)}) collective-permute-start(bf16[328,128]{1,0:T(8,128)(2,1)S(1)} %get-tuple-element.23), channel_id=1, source_target_pairs={{0,2},{2,0},{4,6},{6,4},{8,10},{10,8},{12,14},{14,12},{1,3},{3,1},... | collective-permute-start | bytes 251912 | tf_op jit(solution)/shard_map/ppermute | solution.py:422
  22.5 1.6 %collective-permute-start.3 = (bf16[328,128]{1,0:T(8,128)(2,1)S(1)}, bf16[328,128]{1,0:T(8,128)(2,1)S(1)}, u32[]{:S(2)}, u32[]{:S(2)}) collective-permute-start(bf16[328,128]{1,0:T(8,128)(2,1)S(1)} %get-tuple-element.24), channel_id=1, source_target_pairs={{0,4},{2,6},{4,0},{6,2},{8,12},{10,14},{12,8},{14,10},{1,5},{3,7},... | collective-permute-start | bytes 251912 | tf_op jit(solution)/shard_map/ppermute | solution.py:422
  24.3 1.0 %collective-permute-done.2.refs_1_.refs_5_ = bf16[328,128]{1,0:T(8,128)(2,1)S(1)} collective-permute-done((bf16[328,128]{1,0:T(8,128)(2,1)S(1)}, bf16[328,128]{1,0:T(8,128)(2,1)S(1)}, u32[]{:S(2)}, u32[]{:S(2)}) %collective-permute-start.2) | collective-permute-done | bytes 84000 | tf_op jit(solution)/shard_map/ppermute | solution.py:422
  25.3 2.8 %collective-permute-start.5 = (bf16[328,128]{1,0:T(8,128)(2,1)S(1)}, bf16[328,128]{1,0:T(8,128)(2,1)S(1)}, u32[]{:S(2)}, u32[]{:S(2)}) collective-permute-start(bf16[328,128]{1,0:T(8,128)(2,1)S(1)} %get-tuple-element.26), channel_id=1, source_target_pairs={{0,8},{2,10},{4,12},{6,14},{8,0},{10,2},{12,4},{14,6},{1,9},{3,11}... | collective-permute-start | bytes 251912 | tf_op jit(solution)/shard_map/ppermute | solution.py:422
  28.1 1.4 %collective-permute-start.6 = (bf16[328,128]{1,0:T(8,128)(2,1)S(1)}, bf16[328,128]{1,0:T(8,128)(2,1)S(1)}, u32[]{:S(2)}, u32[]{:S(2)}) collective-permute-start(bf16[328,128]{1,0:T(8,128)(2,1)S(1)} %get-tuple-element.27), channel_id=1, source_target_pairs={{0,10},{2,8},{4,14},{6,12},{8,2},{10,0},{12,6},{14,4},{1,11},{3,9}... | collective-permute-start | bytes 251912 | tf_op jit(solution)/shard_map/ppermute | solution.py:422
  29.5 0.8 %collective-permute-done.4.refs_3_ = bf16[328,128]{1,0:T(8,128)(2,1)S(1)} collective-permute-done((bf16[328,128]{1,0:T(8,128)(2,1)S(1)}, bf16[328,128]{1,0:T(8,128)(2,1)S(1)}, u32[]{:S(2)}, u32[]{:S(2)}) %collective-permute-start.4) | collective-permute-done | bytes 84000 | tf_op jit(solution)/shard_map/ppermute | solution.py:422
  30.4 2.7 %collective-permute-start.7 = (bf16[328,128]{1,0:T(8,128)(2,1)S(1)}, bf16[328,128]{1,0:T(8,128)(2,1)S(1)}, u32[]{:S(2)}, u32[]{:S(2)}) collective-permute-start(bf16[328,128]{1,0:T(8,128)(2,1)S(1)} %get-tuple-element.28), channel_id=1, source_target_pairs={{0,12},{2,14},{4,8},{6,10},{8,4},{10,6},{12,0},{14,2},{1,13},{3,15... | collective-permute-start | bytes 251912 | tf_op jit(solution)/shard_map/ppermute | solution.py:422
  33.0 2.1 %collective-permute-start.8 = (bf16[328,128]{1,0:T(8,128)(2,1)S(1)}, bf16[328,128]{1,0:T(8,128)(2,1)S(1)}, u32[]{:S(2)}, u32[]{:S(2)}) collective-permute-start(bf16[328,128]{1,0:T(8,128)(2,1)S(1)} %get-tuple-element.29), channel_id=1, source_target_pairs={{0,14},{2,12},{4,10},{6,8},{8,6},{10,4},{12,2},{14,0},{1,15},{3,13... | collective-permute-start | bytes 251912 | tf_op jit(solution)/shard_map/ppermute | solution.py:422
  35.1 0.8 %shard_map.131 = (f32[128,256]{1,0:T(8,128)S(1)}, f32[128,256]{1,0:T(8,128)S(1)}, f32[128,256]{1,0:T(8,128)S(1)}, f32[128,256]{1,0:T(8,128)S(1)}) custom-call(bf16[328,128]{1,0:T(8,128)(2,1)S(1)} %get-tuple-element.22.refs_0_.refs_4_, bf16[328,128]{1,0:T(8,128)(2,1)S(1)} %collective-permute-done.2.refs_1_.refs_5_, ...), custom_call_target="tpu_custom_call" | custom-call | tf_op jit(solution)/shard_map/pallas_call | solution.py:431
  36.0 5.1 %collective-permute-done.6.refs_1_.refs_5_ = bf16[328,128]{1,0:T(8,128)(2,1)S(1)} collective-permute-done((bf16[328,128]{1,0:T(8,128)(2,1)S(1)}, bf16[328,128]{1,0:T(8,128)(2,1)S(1)}, u32[]{:S(2)}, u32[]{:S(2)}) %collective-permute-start.6) | collective-permute-done | bytes 84000 | tf_op jit(solution)/shard_map/ppermute | solution.py:422
  41.0 0.8 %shard_map.132 = (f32[128,256]{1,0:T(8,128)S(1)}, f32[128,256]{1,0:T(8,128)S(1)}, f32[128,256]{1,0:T(8,128)S(1)}, f32[128,256]{1,0:T(8,128)S(1)}) custom-call(bf16[328,128]{1,0:T(8,128)(2,1)S(1)} %collective-permute-done.5.refs_0_.refs_4_, bf16[328,128]{1,0:T(8,128)(2,1)S(1)} %collective-permute-done.6.refs_1_.refs_5_, ...), custom_call_target="tpu_custom_call" | custom-call | tf_op jit(solution)/shard_map/pallas_call | solution.py:431
  41.8 3.6 %collective-permute-start.13 = (f32[128,256]{1,0:T(8,128)S(1)}, f32[128,256]{1,0:T(8,128)S(1)}, u32[]{:S(2)}, u32[]{:S(2)}) collective-permute-start(f32[128,256]{1,0:T(8,128)S(1)} %get-tuple-element.35), channel_id=1, source_target_pairs={{0,4},{2,6},{4,0},{6,2},{8,12},{10,14},{12,8},{14,10},{1,5},{3,7},... | collective-permute-start | bytes 393224 | tf_op jit(solution)/shard_map/ppermute | solution.py:443
  45.5 2.0 %collective-permute-start.12 = (f32[128,256]{1,0:T(8,128)S(1)}, f32[128,256]{1,0:T(8,128)S(1)}, u32[]{:S(2)}, u32[]{:S(2)}) collective-permute-start(f32[128,256]{1,0:T(8,128)S(1)} %get-tuple-element.33), channel_id=1, source_target_pairs={{0,4},{2,6},{4,0},{6,2},{8,12},{10,14},{12,8},{14,10},{1,5},{3,7},... | collective-permute-start | bytes 393224 | tf_op jit(solution)/shard_map/ppermute | solution.py:444
  47.5 1.9 %collective-permute-start.17 = (f32[128,256]{1,0:T(8,128)S(1)}, f32[128,256]{1,0:T(8,128)S(1)}, u32[]{:S(2)}, u32[]{:S(2)}) collective-permute-start(f32[128,256]{1,0:T(8,128)S(1)} %shard_map.134), channel_id=1, source_target_pairs={{0,8},{2,10},{4,12},{6,14},{8,0},{10,2},{12,4},{14,6},{1,9},{3,11}... | collective-permute-start | bytes 393224 | tf_op jit(solution)/shard_map/ppermute | solution.py:448
  49.8 3.8 %collective-permute-start.14 = (f32[128,256]{1,0:T(8,128)S(1)}, f32[128,256]{1,0:T(8,128)S(1)}, u32[]{:S(2)}, u32[]{:S(2)}) collective-permute-start(f32[128,256]{1,0:T(8,128)S(1)} %shard_map.133), channel_id=1, source_target_pairs={{0,8},{2,10},{4,12},{6,14},{8,0},{10,2},{12,4},{14,6},{1,9},{3,11}... | collective-permute-start | bytes 393224 | tf_op jit(solution)/shard_map/ppermute | solution.py:448
  54.3 3.9 %collective-permute-done.15.refs_12_ = f32[128,256]{1,0:T(8,128)S(1)} collective-permute-done((f32[128,256]{1,0:T(8,128)S(1)}, f32[128,256]{1,0:T(8,128)S(1)}, u32[]{:S(2)}, u32[]{:S(2)}) %collective-permute-start.15) | collective-permute-done | bytes 131104 | tf_op jit(solution)/shard_map/ppermute | solution.py:444
  58.2 1.6 %collective-permute-done.12.refs_9_ = f32[128,256]{1,0:T(8,128)S(1)} collective-permute-done((f32[128,256]{1,0:T(8,128)S(1)}, f32[128,256]{1,0:T(8,128)S(1)}, u32[]{:S(2)}, u32[]{:S(2)}) %collective-permute-start.12) | collective-permute-done | bytes 131104 | tf_op jit(solution)/shard_map/ppermute | solution.py:444
  59.8 1.2 %attend.1 = bf16[8,32,256]{2,1,0:T(8,128)(2,1)S(1)} custom-call(f32[256,128]{1,0:T(8,128)S(1)} %get-tuple-element.45.cosines, f32[256,128]{1,0:T(8,128)S(1)} %get-tuple-element.46.sines, bf16[328,128]{1,0:T(8,128)(2,1)S(1)} %get-tuple-element.22.refs_0_.refs_4_, bf16[328,128]{1,0:T(8,128)(2,1)S(1)} %collective-permute-done.2.refs_1_.refs_5_, ...), custom_call_target="tpu_custom_call" | custom-call | tf_op jit(solution)/shard_map/attend/pallas_call | solution.py:455
  61.0 13.7 %all_to_all.5.arrived = bf16[8,32,256]{2,1,0:T(8,128)(2,1)S(1)} all-to-all(bf16[8,32,256]{2,1,0:T(8,128)(2,1)S(1)} %attend.1), channel_id=1, replica_groups=mesh['groups'=2,'sp'=8,'fsdp'=2] {'sp'}, dimensions={0} | all-to-all | bytes 262144 | tf_op jit(solution)/shard_map/all_to_all | solution.py:468
  (33 shorter events, 3.2 us)
Async XLA Ops:
  1.9 15.0 %copy-start = (bf16[256]{0:T(256)(128)(2,1)S(1)}, bf16[256]{0:T(256)(128)(2,1)}, u32[]{:S(2)}) copy-start(bf16[256]{0:T(256)(128)(2,1)} %gain_p.1) | copy-start | bytes 1540
  1.9 15.5 %copy-start.1 = (bf16[256]{0:T(256)(128)(2,1)S(1)}, bf16[256]{0:T(256)(128)(2,1)}, u32[]{:S(2)}) copy-start(bf16[256]{0:T(256)(128)(2,1)} %gain_f.1) | copy-start | bytes 1540
  1.9 15.0 %collective-permute-start.9 = (bf16[256,1024]{1,0:T(8,128)(2,1)S(1)}, bf16[256,1024]{1,0:T(8,128)(2,1)S(1)}, u32[]{:S(2)}, u32[]{:S(2)}) collective-permute-start(bf16[256,1024]{1,0:T(8,128)(2,1)S(1)} %get-tuple-element.31), channel_id=1, source_target_pairs={{0,2},{2,0},{4,6},{6,4},{8,10},{10,8},{12,14},{14,12},{1,3},{3,1},... | collective-permute-start | bytes 1572872 | tf_op jit(solution)/shard_map/ppermute | solution.py:392
  5.0 28.1 %collective-permute-start.10 = (bf16[256,1024]{1,0:T(8,128)(2,1)S(1)}, bf16[256,1024]{1,0:T(8,128)(2,1)S(1)}, u32[]{:S(2)}, u32[]{:S(2)}) collective-permute-start(bf16[256,1024]{1,0:T(8,128)(2,1)S(1)} %get-tuple-element.30.refs_6_), channel_id=1, source_target_pairs={{0,1},{1,0},{2,3},{3,2},{4,5},{5,4},{6,7},{7,6},{8,9},{9,8},{10,11... | collective-permute-start | bytes 1572872 | tf_op jit(solution)/shard_map/ppermute | solution.py:423
  16.9 18.2 %collective-permute-start.11 = (bf16[256,1024]{1,0:T(8,128)(2,1)S(1)}, bf16[256,1024]{1,0:T(8,128)(2,1)S(1)}, u32[]{:S(2)}, u32[]{:S(2)}) collective-permute-start(bf16[256,1024]{1,0:T(8,128)(2,1)S(1)} %collective-permute-done.9.refs_7_), channel_id=1, source_target_pairs={{0,1},{1,0},{2,3},{3,2},{4,5},{5,4},{6,7},{7,6},{8,9},{9,8},{10,11... | collective-permute-start | bytes 1572872 | tf_op jit(solution)/shard_map/ppermute | solution.py:424
  16.9 1.9 %collective-permute-start = (bf16[256]{0:T(256)(128)(2,1)S(1)}, bf16[256]{0:T(256)(128)(2,1)S(1)}, u32[]{:S(2)}, u32[]{:S(2)}) collective-permute-start(bf16[256]{0:T(256)(128)(2,1)S(1)} %copy-done), channel_id=1, source_target_pairs={{0,1},{1,0},{2,3},{3,2},{4,5},{5,4},{6,7},{7,6},{8,9},{9,8},{10,11... | collective-permute-start | bytes 1544 | tf_op jit(solution)/shard_map/ppermute | solution.py:393
  17.4 1.4 %collective-permute-start.1 = (bf16[256]{0:T(256)(128)(2,1)S(1)}, bf16[256]{0:T(256)(128)(2,1)S(1)}, u32[]{:S(2)}, u32[]{:S(2)}) collective-permute-start(bf16[256]{0:T(256)(128)(2,1)S(1)} %copy-done.1), channel_id=1, source_target_pairs={{0,1},{1,0},{2,3},{3,2},{4,5},{5,4},{6,7},{7,6},{8,9},{9,8},{10,11... | collective-permute-start | bytes 1544 | tf_op jit(solution)/shard_map/ppermute | solution.py:394
  18.8 0.5 copy-start.2
  18.8 0.5 copy-start.3
  20.7 4.6 %collective-permute-start.2 = (bf16[328,128]{1,0:T(8,128)(2,1)S(1)}, bf16[328,128]{1,0:T(8,128)(2,1)S(1)}, u32[]{:S(2)}, u32[]{:S(2)}) collective-permute-start(bf16[328,128]{1,0:T(8,128)(2,1)S(1)} %get-tuple-element.23), channel_id=1, source_target_pairs={{0,2},{2,0},{4,6},{6,4},{8,10},{10,8},{12,14},{14,12},{1,3},{3,1},... | collective-permute-start | bytes 251912 | tf_op jit(solution)/shard_map/ppermute | solution.py:422
  22.5 5.6 %collective-permute-start.3 = (bf16[328,128]{1,0:T(8,128)(2,1)S(1)}, bf16[328,128]{1,0:T(8,128)(2,1)S(1)}, u32[]{:S(2)}, u32[]{:S(2)}) collective-permute-start(bf16[328,128]{1,0:T(8,128)(2,1)S(1)} %get-tuple-element.24), channel_id=1, source_target_pairs={{0,4},{2,6},{4,0},{6,2},{8,12},{10,14},{12,8},{14,10},{1,5},{3,7},... | collective-permute-start | bytes 251912 | tf_op jit(solution)/shard_map/ppermute | solution.py:422
  24.1 6.3 %collective-permute-start.4 = (bf16[328,128]{1,0:T(8,128)(2,1)S(1)}, bf16[328,128]{1,0:T(8,128)(2,1)S(1)}, u32[]{:S(2)}, u32[]{:S(2)}) collective-permute-start(bf16[328,128]{1,0:T(8,128)(2,1)S(1)} %get-tuple-element.25), channel_id=1, source_target_pairs={{0,6},{2,4},{4,2},{6,0},{8,14},{10,12},{12,10},{14,8},{1,7},{3,5},... | collective-permute-start | bytes 251912 | tf_op jit(solution)/shard_map/ppermute | solution.py:422
  25.3 10.6 %collective-permute-start.5 = (bf16[328,128]{1,0:T(8,128)(2,1)S(1)}, bf16[328,128]{1,0:T(8,128)(2,1)S(1)}, u32[]{:S(2)}, u32[]{:S(2)}) collective-permute-start(bf16[328,128]{1,0:T(8,128)(2,1)S(1)} %get-tuple-element.26), channel_id=1, source_target_pairs={{0,8},{2,10},{4,12},{6,14},{8,0},{10,2},{12,4},{14,6},{1,9},{3,11}... | collective-permute-start | bytes 251912 | tf_op jit(solution)/shard_map/ppermute | solution.py:422
  28.1 12.9 %collective-permute-start.6 = (bf16[328,128]{1,0:T(8,128)(2,1)S(1)}, bf16[328,128]{1,0:T(8,128)(2,1)S(1)}, u32[]{:S(2)}, u32[]{:S(2)}) collective-permute-start(bf16[328,128]{1,0:T(8,128)(2,1)S(1)} %get-tuple-element.27), channel_id=1, source_target_pairs={{0,10},{2,8},{4,14},{6,12},{8,2},{10,0},{12,6},{14,4},{1,11},{3,9}... | collective-permute-start | bytes 251912 | tf_op jit(solution)/shard_map/ppermute | solution.py:422
  30.4 10.7 %collective-permute-start.7 = (bf16[328,128]{1,0:T(8,128)(2,1)S(1)}, bf16[328,128]{1,0:T(8,128)(2,1)S(1)}, u32[]{:S(2)}, u32[]{:S(2)}) collective-permute-start(bf16[328,128]{1,0:T(8,128)(2,1)S(1)} %get-tuple-element.28), channel_id=1, source_target_pairs={{0,12},{2,14},{4,8},{6,10},{8,4},{10,6},{12,0},{14,2},{1,13},{3,15... | collective-permute-start | bytes 251912 | tf_op jit(solution)/shard_map/ppermute | solution.py:422
  33.0 8.0 %collective-permute-start.8 = (bf16[328,128]{1,0:T(8,128)(2,1)S(1)}, bf16[328,128]{1,0:T(8,128)(2,1)S(1)}, u32[]{:S(2)}, u32[]{:S(2)}) collective-permute-start(bf16[328,128]{1,0:T(8,128)(2,1)S(1)} %get-tuple-element.29), channel_id=1, source_target_pairs={{0,14},{2,12},{4,10},{6,8},{8,6},{10,4},{12,2},{14,0},{1,15},{3,13... | collective-permute-start | bytes 251912 | tf_op jit(solution)/shard_map/ppermute | solution.py:422
  35.9 11.6 %collective-permute-start.16 = (f32[128,256]{1,0:T(8,128)S(1)}, f32[128,256]{1,0:T(8,128)S(1)}, u32[]{:S(2)}, u32[]{:S(2)}) collective-permute-start(f32[128,256]{1,0:T(8,128)S(1)} %get-tuple-element.39), channel_id=1, source_target_pairs={{0,4},{2,6},{4,0},{6,2},{8,12},{10,14},{12,8},{14,10},{1,5},{3,7},... | collective-permute-start | bytes 393224 | tf_op jit(solution)/shard_map/ppermute | solution.py:443
  41.8 8.0 %collective-permute-start.13 = (f32[128,256]{1,0:T(8,128)S(1)}, f32[128,256]{1,0:T(8,128)S(1)}, u32[]{:S(2)}, u32[]{:S(2)}) collective-permute-start(f32[128,256]{1,0:T(8,128)S(1)} %get-tuple-element.35), channel_id=1, source_target_pairs={{0,4},{2,6},{4,0},{6,2},{8,12},{10,14},{12,8},{14,10},{1,5},{3,7},... | collective-permute-start | bytes 393224 | tf_op jit(solution)/shard_map/ppermute | solution.py:443
  45.4 12.8 %collective-permute-start.15 = (f32[128,256]{1,0:T(8,128)S(1)}, f32[128,256]{1,0:T(8,128)S(1)}, u32[]{:S(2)}, u32[]{:S(2)}) collective-permute-start(f32[128,256]{1,0:T(8,128)S(1)} %get-tuple-element.37), channel_id=1, source_target_pairs={{0,4},{2,6},{4,0},{6,2},{8,12},{10,14},{12,8},{14,10},{1,5},{3,7},... | collective-permute-start | bytes 393224 | tf_op jit(solution)/shard_map/ppermute | solution.py:444
  45.5 14.3 %collective-permute-start.12 = (f32[128,256]{1,0:T(8,128)S(1)}, f32[128,256]{1,0:T(8,128)S(1)}, u32[]{:S(2)}, u32[]{:S(2)}) collective-permute-start(f32[128,256]{1,0:T(8,128)S(1)} %get-tuple-element.33), channel_id=1, source_target_pairs={{0,4},{2,6},{4,0},{6,2},{8,12},{10,14},{12,8},{14,10},{1,5},{3,7},... | collective-permute-start | bytes 393224 | tf_op jit(solution)/shard_map/ppermute | solution.py:444
  47.5 12.3 %collective-permute-start.17 = (f32[128,256]{1,0:T(8,128)S(1)}, f32[128,256]{1,0:T(8,128)S(1)}, u32[]{:S(2)}, u32[]{:S(2)}) collective-permute-start(f32[128,256]{1,0:T(8,128)S(1)} %shard_map.134), channel_id=1, source_target_pairs={{0,8},{2,10},{4,12},{6,14},{8,0},{10,2},{12,4},{14,6},{1,9},{3,11}... | collective-permute-start | bytes 393224 | tf_op jit(solution)/shard_map/ppermute | solution.py:448
  49.8 10.0 %collective-permute-start.14 = (f32[128,256]{1,0:T(8,128)S(1)}, f32[128,256]{1,0:T(8,128)S(1)}, u32[]{:S(2)}, u32[]{:S(2)}) collective-permute-start(f32[128,256]{1,0:T(8,128)S(1)} %shard_map.133), channel_id=1, source_target_pairs={{0,8},{2,10},{4,12},{6,14},{8,0},{10,2},{12,4},{14,6},{1,9},{3,11}... | collective-permute-start | bytes 393224 | tf_op jit(solution)/shard_map/ppermute | solution.py:448
